TPU v7x, 32 devices: a whole 2x2x4 slice. The times are simulated.
32 devices in a mesh: groups: 2 (over x), tm: 8 (over z, y), rows: 2 (over core).
Axes of the slice: x: 2, y: 2, z: 4, core: 2. Of those that a mesh axis runs over, the one named last changes fastest.
Arguments:
- video_tokens: bfloat16 [32, 32, 32, 1152], P(('groups', 'tm'), 'rows'), parts along dimension 0, may hold values from -6 to 6
- conv_weight: bfloat16 [3, 3, 9, 128, 128], replicated, may hold values from -0.1875 to 0.1875
- point_weight: bfloat16 [1152, 1152], replicated, may hold values from -0.1875 to 0.1875
- depth_weight: bfloat16 [3, 3, 3, 1152], replicated, may hold values from -1.25 to 1.25
- proj_weight: bfloat16 [1152, 8192], P(('tm', 'rows')), may hold values from -0.1875 to 0.1875
- rank_order: int32 [32], P('groups'), parts along dimension 0, may hold values from 0 to 15, each once
Outputs:
- llm_tokens: bfloat16 [4096, 8192], P(('groups', 'tm', 'rows')), parts along dimension 0
There are 2 independent parts, one for each index of `groups`. A program takes and returns all parts, laid end to end along the dimension named above; an argument that names none is the same for every part. Nothing has to cross between parts.
Inputs may be any that keep to these rules, and one draw needn't show every extreme that they name: `rank_order`: each of 0 to 15 appears once.
All inputs are finite; a program needn't handle non-finite values.
Results may differ from a plain program's by a relative error of at most 0.0062.
Values may be sent and summed in bfloat16 or wider, within the bound.
No kernel may reach another device: no remote copies, remote signals or barrier semaphores. Data moves between devices by JAX's collectives and lax.ppermute only.
A program may use at most 192 MiB of HBM per device.

v0:
```python
import itertools
import math

import jax
import jax.numpy as jnp
from jax import lax
from jax.experimental import pallas as pl
from jax.experimental.pallas import tpu as pltpu
from jax.sharding import PartitionSpec as P

AXES = ("groups", "tm", "rows")
SPREAD = 2
CHUNKS = 2


def axes_of():
    groups, count, cores = (lax.axis_size(a) for a in AXES)
    inner = math.gcd(count, SPREAD)
    return groups, count // inner, inner, cores


def place_of():
    _, _, inner, _ = axes_of()
    along = lax.axis_index("tm")
    return lax.axis_index("groups"), along // inner, along % inner, lax.axis_index("rows")


def shifted(value, steps):
    sizes = axes_of()
    if not any(steps):
        return value
    pairs = []
    for source, here in enumerate(itertools.product(*(range(n) for n in sizes))):
        there = [(a + b) % n for a, b, n in zip(here, steps, sizes)]
        target = 0
        for a, n in zip(there, sizes):
            target = target * n + a
        pairs.append((source, target))
    return lax.ppermute(value, AXES, pairs)


def silu(values):
    half = 0.5 * values
    return half + half * jnp.tanh(half)


def normal(values):
    scale = 1.0 / values.shape[-1]
    centred = values - jnp.sum(values, axis=-1, keepdims=True) * scale
    spread = jnp.sum(centred * centred, axis=-1, keepdims=True) * scale
    return centred * lax.rsqrt(spread + 1e-05)


def block_kernel(frame, planes, first, refs):
    if first:
        (x_hbm, up_ref, down_ref, conv_hbm, point_hbm, depth_ref, sent_ref, kept_ref,
         xin, xl, xr, conv_v, point_v, wide, act, rim, sems, conv_sems) = refs
        start_ref, out_refs = None, (sent_ref, kept_ref)
    else:
        (x_hbm, up_ref, down_ref, conv_hbm, point_hbm, depth_ref, start_ref, kept_ref,
         xin, xl, xr, conv_v, point_v, wide, act, rim, sems, conv_sems) = refs
        out_refs = (kept_ref,)
    pairs, _, across, channels = xin.shape
    width = conv_v.shape[-1]
    groups = channels // width
    copies = [
        pltpu.make_async_copy(x_hbm.at[frame], xin.at[pl.ds(1, pairs - 2)], sems.at[0]),
    ]

    def conv_copy(g):
        return pltpu.make_async_copy(conv_hbm.at[:, :, g], conv_v.at[:, :, g], conv_sems.at[g])

    point_copy = pltpu.make_async_copy(point_hbm, point_v, sems.at[3])
    for copy in copies + [conv_copy(g) for g in range(groups)] + [point_copy]:
        copy.start()
    for copy in copies:
        copy.wait()
    core, cores = lax.axis_index("rows"), lax.axis_size("rows")
    blank = jnp.zeros(xin.shape[1:], jnp.bfloat16)
    xin[0] = jnp.where(core == 0, blank, up_ref[frame])
    xin[pairs - 1] = jnp.where(core == cores - 1, blank, down_ref[frame])
    column = lax.broadcasted_iota(jnp.int32, (across, channels), 0)

    def shift(i, carry):
        k, p = i // 2, i % 2
        row = xin[k, p].astype(jnp.float32)
        left = jnp.where(column == 0, 0.0, pltpu.roll(row, 1, 0))
        right = jnp.where(column == across - 1, 0.0, pltpu.roll(row, across - 1, 0))
        xl[k, p] = left.astype(jnp.bfloat16)
        xr[k, p] = right.astype(jnp.bfloat16)
        return carry

    lax.fori_loop(0, 2 * pairs, shift, 0)

    span = pairs - 1
    order = []
    for half in (0, 2):
        order += [(half, 0), (half, 1), (half + 1, 0), (half + 1, 1), (half, 2), (half + 1, 2)]
    sources = (xl, xin, xr)
    zero = jnp.zeros((width, width), jnp.bfloat16)

    def convolve(g, carry):
        lanes = pl.ds(pl.multiple_of(g * width, width), width)
        conv_copy(g).wait()
        left_side, right_side = [], []
        for a, b in order:
            piece = sources[b][pl.ds(a // 2, span), a % 2, :, lanes]
            left_side.append(piece.reshape(span * across, width))
            taps = [conv_v[a - j, b, g] if 0 <= a - j < 3 else zero for j in range(2)]
            right_side.append(jnp.concatenate(taps, axis=1))
        out = jnp.dot(
            jnp.concatenate(left_side, axis=1),
            jnp.concatenate(right_side, axis=0),
            preferred_element_type=jnp.float32,
        )
        for j in range(2):
            wide[:, j, :, lanes] = out[:, j * width : (j + 1) * width].reshape(span, across, width)
        return carry

    lax.fori_loop(0, groups, convolve, 0)

    def activate(i, carry):
        for p in range(2):
            for h in range(0, across, 16):
                act[i, p, pl.ds(h, 16)] = silu(normal(wide[i, p, pl.ds(h, 16)])).astype(jnp.bfloat16)
        return carry

    lax.fori_loop(0, span, activate, 0, unroll=3)
    point_copy.wait()
    step = 2 * width

    def mix(at, lanes):
        product = jnp.dot(
            act[...].reshape(2 * span * across, channels),
            point_v[:, lanes],
            preferred_element_type=jnp.float32,
        )
        wide[:, :, :, lanes] = product.reshape(span, 2, across, product.shape[1])
        return at

    lax.fori_loop(0, channels // step, lambda n, t: mix(t, pl.ds(pl.multiple_of(n * step, step), step)), 0, unroll=True)
    if channels % step:
        mix(0, pl.ds(channels // step * step, channels % step))

    margin = rim.shape[2] - across
    keep = jnp.where(core == 0, 0.0, 1.0)

    def finish(i, carry):
        for p in range(2):
            for h in range(0, across, 16):
                value = xin[i + p, 1 - p, pl.ds(h, 16)].astype(jnp.float32)
                value = silu(value + normal(wide[i, p, pl.ds(h, 16)]))
                if p == 0:
                    value = jnp.where(i == 0, value * keep, value)
                for g in range(groups):
                    rim[g, 2 * i + p, pl.ds(margin + h, 16), :] = value[:, g * width : (g + 1) * width]
            for g in range(groups):
                rim[g, 2 * i + p, pl.ds(0, margin), :] = jnp.zeros((margin, width), jnp.float32)
        return carry

    lax.fori_loop(0, span, finish, 0, unroll=3)

    half = across // 2

    def sample_group(g, outer):
        lanes = pl.ds(pl.multiple_of(g * width, width), width)
        weights = [
            [
                jnp.broadcast_to(
                    depth_ref[plane, tap // 3, pl.ds(tap % 3, 1), lanes].astype(jnp.float32), (8, width)
                )
                for tap in range(9)
            ]
            for plane in planes
        ]

        def sample(p, carry):
            for t in range(half // 8):
                where = pl.ds(pl.multiple_of(p * half + 8 * t, 8), 8)
                totals = [None] * len(planes)
                if start_ref is not None:
                    totals[0] = start_ref[where, lanes]
                for b in range(3):
                    for e in range(3):
                        value = rim[g, 2 * p + b, pl.ds(margin - 1 + e + 16 * t, 8, 2), :]
                        for n in range(len(planes)):
                            term = weights[n][3 * b + e] * value
                            totals[n] = term if totals[n] is None else totals[n] + term
                for ref, total in zip(out_refs, totals):
                    ref[where, lanes] = total.astype(ref.dtype)
            return carry

        lax.fori_loop(0, span - 1, sample, 0, unroll=2)
        return outer

    lax.fori_loop(0, groups, sample_group, 0)


def block_call(frame, x, up, down, conv_weight, point_weight, depth_weight, start=None):
    first = start is None
    _, near, _, across, channels = x.shape
    pairs = near + 2
    span = pairs - 1
    groups, width = conv_weight.shape[2:4]
    count = near * (across // 2)
    out = jax.ShapeDtypeStruct((count, channels), jnp.float32)
    anywhere = pl.BlockSpec(memory_space=pltpu.HBM)
    vmem = pl.BlockSpec(memory_space=pltpu.VMEM)
    args = [x, up, down, conv_weight, point_weight, depth_weight] + ([] if first else [start])
    planes = (0, 2) if first else (1,)
    return pl.pallas_call(
        lambda *refs: block_kernel(frame, planes, first, refs),
        out_shape=[jax.ShapeDtypeStruct(out.shape, jnp.bfloat16), out] if first else out,
        in_specs=[anywhere, vmem, vmem, anywhere, anywhere] + [vmem] * (1 if first else 2),
        out_specs=[vmem, vmem] if first else vmem,
        scratch_shapes=[
            pltpu.VMEM((pairs, 2, across, channels), jnp.bfloat16),
            pltpu.VMEM((pairs, 2, across, channels), jnp.bfloat16),
            pltpu.VMEM((pairs, 2, across, channels), jnp.bfloat16),
            pltpu.VMEM(conv_weight.shape, jnp.bfloat16),
            pltpu.VMEM(point_weight.shape, jnp.bfloat16),
            pltpu.VMEM((span, 2, across, channels), jnp.float32),
            pltpu.VMEM((span, 2, across, channels), jnp.bfloat16),
            pltpu.VMEM((groups, 2 * span, across + 8, width), jnp.float32),
            pltpu.SemaphoreType.DMA((4,)),
            pltpu.SemaphoreType.DMA((groups,)),
        ],
        compiler_params=pltpu.CompilerParams(vmem_limit_bytes=60 << 20),
        name="block_last" if first else "block_first",
    )(*args)


HBM = pl.BlockSpec(memory_space=pltpu.HBM)
VMEM = pl.BlockSpec(memory_space=pltpu.VMEM)
SMEM = pl.BlockSpec(memory_space=pltpu.SMEM)


def run_copies(copies):
    for copy in copies:
        copy.start()
    for copy in copies:
        copy.wait()


def cut_kernel(weight_ref, x_ref, *refs):
    _, _, inner, cores = axes_of()
    g, _, y, c = place_of()
    head, tail, pieces, sem = refs[0], refs[1], refs[2:-1], refs[-1]
    block = pieces[0].shape[1]
    near = x_ref.shape[1]
    copies = [
        pltpu.make_async_copy(x_ref.at[:, 0], head, sem.at[len(pieces)]),
        pltpu.make_async_copy(x_ref.at[:, near - 1], tail, sem.at[len(pieces) + 1]),
    ]
    for n, (dy, dc) in enumerate(itertools.product(range(inner), range(cores))):
        to = (g * inner + lax.rem(y + dy, inner)) * cores + lax.rem(c + dc, cores)
        lanes = pl.ds(pl.multiple_of(to * block, 128), block)
        copies.append(pltpu.make_async_copy(weight_ref.at[:, lanes], pieces[n], sem.at[n]))
    run_copies(copies)


def join_kernel(*refs):
    _, _, inner, cores = axes_of()
    _, _, y, c = place_of()
    pieces, level_ref = refs[:-1], refs[-1]
    depth = pieces[0].shape[0]
    for n, (dy, dc) in enumerate(itertools.product(range(inner), range(cores))):
        source = lax.rem(y + inner - dy, inner) * cores + lax.rem(c + cores - dc, cores)
        level_ref[pl.ds(pl.multiple_of(source * depth, 8), depth), :] = pieces[n][...]


def cut(proj_weight, paired):
    groups, _, inner, cores = axes_of()
    g, _, y, c = place_of()
    depth, width = proj_weight.shape
    block = width // (groups * inner * cores)
    steps = list(itertools.product(range(inner), range(cores)))
    if depth % 8 or block % 128:
        to = [(g * inner + (y + dy) % inner) * cores + (c + dc) % cores for dy, dc in steps]
        pieces = [lax.dynamic_slice_in_dim(proj_weight, t * block, block, axis=1) for t in to]
        return paired[:, 0], paired[:, -1], pieces
    edge = jax.ShapeDtypeStruct(paired.shape[:1] + paired.shape[2:], paired.dtype)
    head, tail, *pieces = pl.pallas_call(
        cut_kernel,
        out_shape=[edge, edge] + [jax.ShapeDtypeStruct((depth, block), proj_weight.dtype)] * len(steps),
        in_specs=[HBM, HBM],
        out_specs=[VMEM] * (len(steps) + 2),
        scratch_shapes=[pltpu.SemaphoreType.DMA((len(steps) + 2,))],
        compiler_params=pltpu.CompilerParams(vmem_limit_bytes=60 << 20),
        name="cut",
    )(proj_weight, paired)
    return head, tail, pieces


def walk(outer):
    pairs = [n ^ 1 if n ^ 1 < outer else n for n in range(outer)]
    links = [((n - 1) ^ 1) + 1 if 0 < n and ((n - 1) ^ 1) + 1 < outer else n for n in range(outer)]
    own = list(range(outer))
    moves, pieces = [], [own]
    last = {"pairs": 0, "links": 0}
    missing = [set(own) - {n} for n in own]
    stage = 1
    while any(missing):
        done = dict(last)
        for name, other, perm in (("pairs", "links", pairs), ("links", "pairs", links)):
            source = done[other] if stage > 1 else 0
            if source is None:
                continue
            got = [pieces[source][perm[n]] for n in own]
            if not any(got[n] in missing[n] for n in own):
                last[name] = None
                continue
            moves.append((stage, source, perm))
            pieces.append(got)
            last[name] = len(pieces) - 1
            for n in own:
                missing[n].discard(got[n])
        stage += 1
    return moves, pieces


def slot_of(pieces, n, z):
    outer = len(pieces[0])
    slot = 0
    for here in range(outer):
        fresh = all(pieces[m][here] != pieces[n][here] for m in range(n))
        slot = jnp.where(z == here, pieces[n][here] if fresh else -1, slot)
    return slot


def fast(block, outer, peers, count):
    share = count // (outer * peers)
    return share % 8 == 0 and lax.axis_size("rows") * share % 16 == 0 and block % (256 * CHUNKS) == 0


def spread_weight(pieces, count):
    _, outer, inner, cores = axes_of()
    _, _, y, c = place_of()
    depth, block = pieces[0].shape
    steps = list(itertools.product(range(inner), range(cores)))
    pieces = [shifted(piece, (0, 0, dy, dc)) for piece, (dy, dc) in zip(pieces, steps)]
    rows = len(steps) * depth
    if depth % 8 == 0 and block % 128 == 0:
        level = pl.pallas_call(
            join_kernel,
            out_shape=jax.ShapeDtypeStruct((rows, block), pieces[0].dtype),
            in_specs=[VMEM] * len(steps),
            out_specs=VMEM,
            compiler_params=pltpu.CompilerParams(vmem_limit_bytes=8 << 20),
            name="join",
        )(*pieces)
    else:
        level = jnp.zeros((rows, block), pieces[0].dtype)
        for piece, (dy, dc) in zip(pieces, steps):
            at = ((y - dy) % inner) * cores + (c - dc) % cores
            level = lax.dynamic_update_slice_in_dim(level, piece, at * depth, axis=0)
    fits = fast(block, outer, len(steps), count)
    chunks = CHUNKS if fits else 1
    moves = walk(outer)[0]
    levels = [[level] for _ in range(chunks)]
    for stage, source, perm in moves:
        whole = [(n * inner + m, perm[n] * inner + m) for n in range(outer) for m in range(inner)]
        width = block if stage == 1 else block // chunks
        for h in range(chunks if stage > 1 else 1):
            value = levels[h][source]
            if value.shape[1] != width:
                value = value[:, h * width : (h + 1) * width]
            value = lax.ppermute(value, "tm", whole)
            for to in range(chunks) if stage == 1 else [h]:
                levels[to].append(value)
    return levels


def project_kernel(chunk, outer, inner, cores, *refs):
    peers = inner * cores
    held = walk(outer)[1]
    x_refs, refs = refs[:peers], refs[peers:]
    w_refs, refs = refs[: len(held)], refs[len(held) :]
    out_refs, (xs, ws, product, x_sem, w_sem) = refs[:peers], refs[peers:]
    _, z, y, c = place_of()
    count = x_refs[0].shape[0]
    rows, block = ws.shape[0] // outer, ws.shape[1]
    share = count // (outer * peers)
    w_refs = [
        w if w.shape[1] == block else w.at[:, pl.ds(chunk * block, block)] for w in w_refs
    ]
    for n, x_ref in enumerate(x_refs):
        pltpu.make_async_copy(x_ref, xs.at[pl.ds(n * count, count)], x_sem.at[n]).start()
    for n, w_ref in enumerate(w_refs):
        slot = slot_of(held, n, z)

        @pl.when(slot >= 0)
        def _():
            into = ws.at[pl.ds(pl.multiple_of(slot * rows, 16), rows)]
            pltpu.make_async_copy(w_ref, into, w_sem.at[n]).start()

    for n, x_ref in enumerate(x_refs):
        pltpu.make_async_copy(x_ref, xs.at[pl.ds(n * count, count)], x_sem.at[n]).wait()
    for n, w_ref in enumerate(w_refs):
        slot = slot_of(held, n, z)

        @pl.when(slot >= 0)
        def _():
            into = ws.at[pl.ds(pl.multiple_of(slot * rows, 16), rows)]
            pltpu.make_async_copy(w_ref, into, w_sem.at[n]).wait()

    def multiply(n, carry):
        lanes = pl.ds(pl.multiple_of(n * 256, 256), 256)
        out = jnp.dot(xs[...], ws[:, lanes], preferred_element_type=jnp.float32)
        product[:, :, :, :, lanes] = out.reshape(peers, outer, peers, share, 256)
        return carry

    lax.fori_loop(0, block // 256, multiply, 0)
    for n, (ty, tc) in enumerate(itertools.product(range(inner), range(cores))):
        target = lax.rem(y + ty, inner) * cores + lax.rem(c + tc, cores)
        for dz, dy in itertools.product(range(outer), range(inner)):
            from_z, from_y = lax.rem(z + outer - dz, outer), lax.rem(y + inner - dy, inner)
            tiles = []
            for from_c in range(cores):
                dc = lax.rem(c + cores - from_c, cores)
                tiles.append(product[dy * cores + dc, dz, target])
            at = (from_z * inner + from_y) * cores * share
            tile = jnp.concatenate(tiles, axis=0).astype(jnp.bfloat16)
            out_refs[n][pl.ds(pl.multiple_of(at, cores * share), cores * share), :] = tile


def project_call(chunk, blocks, levels, outer, inner, cores):
    peers = inner * cores
    count, channels = blocks[0].shape
    rows, block = levels[0].shape
    block //= CHUNKS
    share = count // (outer * peers)
    return pl.pallas_call(
        lambda *refs: project_kernel(chunk, outer, inner, cores, *refs),
        out_shape=[jax.ShapeDtypeStruct((count, block), jnp.bfloat16)] * peers,
        in_specs=[HBM] * (peers + len(levels)),
        out_specs=[VMEM] * peers,
        scratch_shapes=[
            pltpu.VMEM((peers * count, channels), jnp.bfloat16),
            pltpu.VMEM((outer * rows, block), jnp.bfloat16),
            pltpu.VMEM((peers, outer, peers, share, block), jnp.float32),
            pltpu.SemaphoreType.DMA((peers,)),
            pltpu.SemaphoreType.DMA((len(levels),)),
        ],
        compiler_params=pltpu.CompilerParams(vmem_limit_bytes=32 << 20),
        name="project",
    )(*blocks, *levels)


def project_plain(chunk, blocks, levels, outer, inner, cores):
    _, z, y, c = place_of()
    peers = inner * cores
    count, channels = blocks[0].shape
    block = levels[0].shape[1]
    share = count // (outer * peers)
    held = walk(outer)[1]
    whole = jnp.zeros((outer,) + levels[0].shape, levels[0].dtype)
    for n, level in enumerate(levels):
        slot = slot_of(held, n, z)
        at = jnp.maximum(slot, 0)
        kept = lax.dynamic_index_in_dim(whole, at, 0, False)
        level = jnp.where(slot >= 0, level, kept)
        whole = lax.dynamic_update_slice_in_dim(whole, level[None], at, axis=0)
    every = jnp.zeros((inner, cores, outer, peers, share, channels), jnp.bfloat16)
    for n, (dy, dc) in enumerate(itertools.product(range(inner), range(cores))):
        piece = blocks[n].reshape(outer, peers, share, channels)
        piece = jnp.roll(piece[(-jnp.arange(outer)) % outer], z, axis=0)
        every = lax.dynamic_update_slice(
            every, piece[None, None], ((y - dy) % inner, (c - dc) % cores, 0, 0, 0, 0)
        )
    every = jnp.transpose(every, (3, 2, 0, 1, 4, 5)).reshape(-1, channels)
    product = jnp.dot(every, whole.reshape(-1, block), preferred_element_type=jnp.float32)
    product = product.astype(jnp.bfloat16).reshape(peers, count, block)
    return [
        lax.dynamic_index_in_dim(product, ((y + ty) % inner) * cores + (c + tc) % cores, 0, False)
        for ty, tc in itertools.product(range(inner), range(cores))
    ]


def collect_kernel(*refs):
    groups, _, inner, cores = axes_of()
    g, _, y, c = place_of()
    pieces, out_ref, sem = refs[:-2], refs[-2], refs[-1]
    block = pieces[0].shape[1]
    chunks = len(pieces) // (groups * inner * cores)
    copies = []
    where = itertools.product(range(groups), range(inner), range(cores), range(chunks))
    for n, (dg, dy, dc, h) in enumerate(where):
        source = lax.rem(g + groups - dg, groups) * inner + lax.rem(y + inner - dy, inner)
        source = source * cores + lax.rem(c + cores - dc, cores)
        lanes = pl.ds(pl.multiple_of((source * chunks + h) * block, 128), block)
        copies.append(pltpu.make_async_copy(pieces[n], out_ref.at[:, lanes], sem.at[n]))
    run_copies(copies)


def deliver(placed, levels):
    groups, outer, inner, cores = axes_of()
    g, _, y, c = place_of()
    count, _ = placed.shape
    block = levels[0][0].shape[1]
    part = count // outer
    mine = [shifted(placed[dz * part : (dz + 1) * part], (0, dz, 0, 0)) for dz in range(outer)]
    mine = jnp.concatenate(mine, axis=0)
    chips = {}
    for dg, dy in itertools.product(reversed(range(groups)), reversed(range(inner))):
        chips[dg, dy] = shifted(mine, (dg, 0, dy, 0))
    blocks = {}
    for dg, dy, dc in itertools.product(range(groups), range(inner), range(cores)):
        blocks[dg, dy, dc] = shifted(chips[dg, dy], (0, 0, 0, dc))
    fits = fast(block, outer, inner * cores, count)
    call = project_call if fits else project_plain
    steps = list(itertools.product(range(inner), range(cores)))
    arrived = {}
    for h, held in enumerate(levels):
        for dg in reversed(range(groups)):
            group = [blocks[dg, dy, dc] for dy, dc in steps]
            pieces = call(h, group, held, outer, inner, cores)
            for (dy, dc), piece in zip(steps, pieces):
                arrived[dg, dy, dc, h] = shifted(piece, (dg, 0, dy, dc))
    if fits:
        pieces = [piece for _, piece in sorted(arrived.items())]
        return pl.pallas_call(
            collect_kernel,
            out_shape=jax.ShapeDtypeStruct((count, len(pieces) // len(levels) * block), jnp.bfloat16),
            in_specs=[VMEM] * len(pieces),
            out_specs=HBM,
            scratch_shapes=[pltpu.SemaphoreType.DMA((len(pieces),))],
            compiler_params=pltpu.CompilerParams(vmem_limit_bytes=8 << 20),
            name="collect",
        )(*pieces)
    out = jnp.zeros((count, groups * inner * cores * block), jnp.bfloat16)
    for (dg, dy, dc, _), piece in sorted(arrived.items()):
        source = (((g - dg) % groups) * inner + (y - dy) % inner) * cores + (c - dc) % cores
        out = lax.dynamic_update_slice_in_dim(out, piece, source * block, axis=1)
    return out


def place_kernel(spans, sum_ref, rim_ref, target_ref, placed_ref):
    count = sum_ref.shape[0]
    rim = rim_ref[...].astype(jnp.float32)
    row = lax.broadcasted_iota(jnp.int32, rim.shape, 0)
    rim = jnp.where((row < count // spans) & (lax.axis_index("tm") == 0), 0.0, rim)
    tokens = silu(sum_ref[...] + rim).astype(jnp.bfloat16)
    slot = lax.broadcasted_iota(jnp.int32, (count, count), 0)
    selector = jnp.where(slot == target_ref[...], 1.0, 0.0).astype(jnp.bfloat16)
    placed = jnp.dot(selector, tokens, preferred_element_type=jnp.float32)
    placed_ref[...] = placed.astype(jnp.bfloat16)


def place_call(spans, total, rim, target):
    vmem = pl.BlockSpec(memory_space=pltpu.VMEM)
    return pl.pallas_call(
        lambda *refs: place_kernel(spans, *refs),
        out_shape=jax.ShapeDtypeStruct(total.shape, jnp.bfloat16),
        in_specs=[vmem] * 3,
        out_specs=vmem,
        compiler_params=pltpu.CompilerParams(vmem_limit_bytes=8 << 20),
        name="place",
    )(total, rim, target)


def slots(rank_order, count):
    _, outer, inner, cores = axes_of()
    _, z, _, _ = place_of()
    ranks = outer * inner * cores
    period = 2 * ranks
    share = count // ranks
    position = jnp.arange(count, dtype=jnp.int32)
    stripe = position % period
    folded = jnp.minimum(stripe, period - 1 - stripe)
    one_hot = folded[:, None] == jnp.arange(ranks, dtype=jnp.int32)[None, :]
    owner = jnp.sum(jnp.where(one_hot, rank_order[None, :], 0), axis=1)
    owner = (owner + (outer - z) * inner * cores) % ranks
    target = owner * share + (position // period) * 2 + (stripe >= ranks).astype(jnp.int32)
    return target.reshape(1, count)


def local(video_tokens, conv_weight, point_weight, depth_weight, proj_weight, rank_order):
    frames, height, across, channels = video_tokens.shape
    cores, along = lax.axis_size("rows"), lax.axis_size("tm")
    paired = video_tokens.reshape(frames, height // 2, 2, across, channels)
    head, tail, pieces = cut(proj_weight, paired)
    up = lax.ppermute(tail, "rows", [(i, (i + 1) % cores) for i in range(cores)])
    down = lax.ppermute(head, "rows", [((i + 1) % cores, i) for i in range(cores)])
    levels = spread_weight(pieces, frames // 2 * (height // 2) * (across // 2))
    shared = (paired, up, down, conv_weight, point_weight, depth_weight)
    sums, rims = [], []
    for o in reversed(range(frames // 2)):
        sent, kept = block_call(2 * o + 1, *shared)
        rims.insert(0, sent)
        sums.insert(0, block_call(2 * o, *shared, kept))
    rim = lax.ppermute(rims[-1], "tm", [(i, (i + 1) % along) for i in range(along)])
    if frames > 2:
        rim = jnp.concatenate([rim] + rims[:-1], axis=0)
    total = sums[0] if len(sums) == 1 else jnp.concatenate(sums, axis=0)
    placed = place_call(frames // 2, total, rim, slots(rank_order, total.shape[0]))
    return deliver(placed, levels)


def solution(mesh):
    return jax.shard_map(
        local,
        mesh=mesh,
        in_specs=(
            P(("groups", "tm"), "rows", None, None),
            P(),
            P(),
            P(),
            P(("tm", "rows"), None),
            P("groups"),
        ),
        out_specs=P(("groups", "tm", "rows"), None),
        check_vma=False,
    )
```

profile of v0, /device:TPU:0, one launch (start us, length us, event | category | flops | bytes accessed | tf_op | source)
XLA Modules:
  0.0 121.6 jit_solution(14771852593429945294)
XLA Ops:
  0.0 2.3 %cut.1 = (bf16[2,2,32,1152]{3,2,1,0:T(8,128)(2,1)}, bf16[2,2,32,1152]{3,2,1,0:T(8,128)(2,1)}, bf16[72,1024]{1,0:T(8,128)(2,1)}, bf16[72,1024]{1,0:T(8,128)(2,1)}...) custom-call(bf16[72,8192]{1,0:T(8,128)(2,1)} %weight_ref.1, bf16[2,8,2,32,1152]{4,3,2,1,0:T(8,128)(2,1)} %bitcast.3), custom_call_target="tpu_custom_call" | custom-call | tf_op jit(solution)/shard_map/cut/pallas_call | solution.py:283
  2.9 2.9 %collective-permute-start.10 = (bf16[72,1024]{1,0:T(8,128)(2,1)}, bf16[72,1024]{1,0:T(8,128)(2,1)S(1)}, u32[]{:S(2)}, u32[]{:S(2)}) collective-permute-start(bf16[72,1024]{1,0:T(8,128)(2,1)} %get-tuple-element.35), channel_id=1, source_target_pairs={{0,2},{1,3},{2,0},{3,1},{4,6},{5,7},{6,4},{7,5},{8,10},{9,11},{10,... | collective-permute-start | bytes 442376 | tf_op jit(solution)/shard_map/ppermute | solution.py:39
  7.4 14.2 %block_last.1 = (bf16[128,1152]{1,0:T(8,128)(2,1)}, f32[128,1152]{1,0:T(8,128)}) custom-call(bf16[2,8,2,32,1152]{4,3,2,1,0:T(8,128)(2,1)} %bitcast.4, bf16[2,2,32,1152]{3,2,1,0:T(8,128)(2,1)} %copy-done.2, bf16[2,2,32,1152]{3,2,1,0:T(8,128)(2,1)} %copy-done.3, bf16[3,3,9,128,128]{4,3,2,1,0:T(8,128)(2,1)} %refs_3_.3, bf16[1152,1152]{1,0:T(8,128)(2,1)} %refs_4_.3, ...), custom_call_target="tpu_custom_call" | custom-call | tf_op jit(solution)/shard_map/block_last/pallas_call | solution.py:211
  21.6 2.1 %collective-permute-start.2 = (bf16[128,1152]{1,0:T(8,128)(2,1)}, bf16[128,1152]{1,0:T(8,128)(2,1)S(1)}, u32[]{:S(2)}, u32[]{:S(2)}) collective-permute-start(bf16[128,1152]{1,0:T(8,128)(2,1)} %get-tuple-element.32), channel_id=1, source_target_pairs={{0,2},{2,4},{4,6},{6,8},{8,10},{10,12},{12,14},{14,0},{1,3},{3,5},... | collective-permute-start | bytes 884744 | tf_op jit(solution)/shard_map/ppermute | solution.py:592
  23.9 1.6 %collective-permute-start.12 = (bf16[288,1024]{1,0:T(8,128)(2,1)S(1)}, bf16[288,1024]{1,0:T(8,128)(2,1)S(1)}, u32[]{:S(2)}, u32[]{:S(2)}) collective-permute-start(bf16[288,1024]{1,0:T(8,128)(2,1)S(1)} %join.1.refs_4_), channel_id=1, source_target_pairs={{0,4},{2,6},{4,0},{6,2},{8,12},{10,14},{12,8},{14,10},{1,5},{3,7},... | collective-permute-start | bytes 1769480 | tf_op jit(solution)/shard_map/ppermute | solution.py:368
  26.3 14.1 %block_first.1.refs_0_ = f32[128,1152]{1,0:T(8,128)} custom-call(bf16[2,8,2,32,1152]{4,3,2,1,0:T(8,128)(2,1)} %bitcast.5, bf16[2,2,32,1152]{3,2,1,0:T(8,128)(2,1)} %copy-done.2, bf16[2,2,32,1152]{3,2,1,0:T(8,128)(2,1)} %copy-done.3, bf16[3,3,9,128,128]{4,3,2,1,0:T(8,128)(2,1)} %refs_3_.3, bf16[1152,1152]{1,0:T(8,128)(2,1)} %refs_4_.3, ...), custom_call_target="tpu_custom_call" | custom-call | tf_op jit(solution)/shard_map/block_first/pallas_call | solution.py:211
  41.8 4.4 %collective-permute-start.3 = (bf16[32,1152]{1,0:T(8,128)(2,1)S(1)}, bf16[32,1152]{1,0:T(8,128)(2,1)S(1)}, u32[]{:S(2)}, u32[]{:S(2)}) collective-permute-start(bf16[32,1152]{1,0:T(8,128)(2,1)S(1)} %get-tuple-element.60), channel_id=1, source_target_pairs={{0,4},{1,5},{2,6},{3,7},{4,8},{5,9},{6,10},{7,11},{8,12},{9,13},{1... | collective-permute-start | bytes 221192 | tf_op jit(solution)/shard_map/ppermute | solution.py:39
  46.2 2.4 %collective-permute-start.5 = (bf16[32,1152]{1,0:T(8,128)(2,1)S(1)}, bf16[32,1152]{1,0:T(8,128)(2,1)S(1)}, u32[]{:S(2)}, u32[]{:S(2)}) collective-permute-start(bf16[32,1152]{1,0:T(8,128)(2,1)S(1)} %get-tuple-element.58), channel_id=1, source_target_pairs={{0,12},{1,13},{2,14},{3,15},{4,0},{5,1},{6,2},{7,3},{8,4},{9,5},{1... | collective-permute-start | bytes 221192 | tf_op jit(solution)/shard_map/ppermute | solution.py:39
  48.7 3.7 %collective-permute-done.4 = bf16[32,1152]{1,0:T(8,128)(2,1)S(1)} collective-permute-done((bf16[32,1152]{1,0:T(8,128)(2,1)S(1)}, bf16[32,1152]{1,0:T(8,128)(2,1)S(1)}, u32[]{:S(2)}, u32[]{:S(2)}) %collective-permute-start.4) | collective-permute-done | bytes 73760 | tf_op jit(solution)/shard_map/ppermute | solution.py:39
  56.7 3.0 %collective-permute-start.17 = (bf16[288,512]{1,0:T(8,128)(2,1)S(1)}, bf16[288,512]{1,0:T(8,128)(2,1)S(1)}, u32[]{:S(2)}, u32[]{:S(2)}) collective-permute-start(bf16[288,512]{1,0:T(8,128)(2,1)S(1)} %get-tuple-element.55), channel_id=1, source_target_pairs={{0,4},{2,6},{4,0},{6,2},{8,12},{10,14},{12,8},{14,10},{1,5},{3,7},... | collective-permute-start | bytes 884744 | tf_op jit(solution)/shard_map/ppermute | solution.py:368
  59.7 2.2 %collective-permute-done.26.refs_0_ = bf16[128,1152]{1,0:T(8,128)(2,1)S(1)} collective-permute-done((bf16[128,1152]{1,0:T(8,128)(2,1)S(1)}, bf16[128,1152]{1,0:T(8,128)(2,1)S(1)}, u32[]{:S(2)}, u32[]{:S(2)}) %collective-permute-start.26) | collective-permute-done | bytes 294944 | tf_op jit(solution)/shard_map/ppermute | solution.py:39
  62.6 4.6 %collective-permute-done.28.refs_2_ = bf16[128,1152]{1,0:T(8,128)(2,1)S(1)} collective-permute-done((bf16[128,1152]{1,0:T(8,128)(2,1)S(1)}, bf16[128,1152]{1,0:T(8,128)(2,1)S(1)}, u32[]{:S(2)}, u32[]{:S(2)}) %collective-permute-start.28) | collective-permute-done | bytes 294944 | tf_op jit(solution)/shard_map/ppermute | solution.py:39
  68.6 2.1 %collective-permute-start.19 = (bf16[288,512]{1,0:T(8,128)(2,1)S(1)}, bf16[288,512]{1,0:T(8,128)(2,1)S(1)}, u32[]{:S(2)}, u32[]{:S(2)}) collective-permute-start(bf16[288,512]{1,0:T(8,128)(2,1)S(1)} %collective-permute-done.18.refs_8_), channel_id=1, source_target_pairs={{0,4},{2,6},{4,0},{6,2},{8,12},{10,14},{12,8},{14,10},{1,5},{3,7},... | collective-permute-start | bytes 884744 | tf_op jit(solution)/shard_map/ppermute | solution.py:368
  71.0 1.7 %collective-permute-start.14 = (bf16[288,512]{1,0:T(8,128)(2,1)S(1)}, bf16[288,512]{1,0:T(8,128)(2,1)S(1)}, u32[]{:S(2)}, u32[]{:S(2)}) collective-permute-start(bf16[288,512]{1,0:T(8,128)(2,1)S(1)} %get-tuple-element.56), channel_id=1, source_target_pairs={{0,4},{2,6},{4,0},{6,2},{8,12},{10,14},{12,8},{14,10},{1,5},{3,7},... | collective-permute-start | bytes 884744 | tf_op jit(solution)/shard_map/ppermute | solution.py:368
  73.0 5.6 %collective-permute-done.19.refs_9_ = bf16[288,512]{1,0:T(8,128)(2,1)S(1)} collective-permute-done((bf16[288,512]{1,0:T(8,128)(2,1)S(1)}, bf16[288,512]{1,0:T(8,128)(2,1)S(1)}, u32[]{:S(2)}, u32[]{:S(2)}) %collective-permute-start.19) | collective-permute-done | bytes 294944 | tf_op jit(solution)/shard_map/ppermute | solution.py:368
  81.7 3.3 %collective-permute-done.14.refs_7_ = bf16[288,512]{1,0:T(8,128)(2,1)S(1)} collective-permute-done((bf16[288,512]{1,0:T(8,128)(2,1)S(1)}, bf16[288,512]{1,0:T(8,128)(2,1)S(1)}, u32[]{:S(2)}, u32[]{:S(2)}) %collective-permute-start.14) | collective-permute-done | bytes 294944 | tf_op jit(solution)/shard_map/ppermute | solution.py:368
  86.0 5.1 %collective-permute-done.16.refs_9_ = bf16[288,512]{1,0:T(8,128)(2,1)S(1)} collective-permute-done((bf16[288,512]{1,0:T(8,128)(2,1)S(1)}, bf16[288,512]{1,0:T(8,128)(2,1)S(1)}, u32[]{:S(2)}, u32[]{:S(2)}) %collective-permute-start.16) | collective-permute-done | bytes 294944 | tf_op jit(solution)/shard_map/ppermute | solution.py:368
  97.0 1.9 %collective-permute-start.34 = (bf16[128,512]{1,0:T(8,128)(2,1)S(1)}, bf16[128,512]{1,0:T(8,128)(2,1)S(1)}, u32[]{:S(2)}, u32[]{:S(2)}) collective-permute-start(bf16[128,512]{1,0:T(8,128)(2,1)S(1)} %get-tuple-element.49), channel_id=1, source_target_pairs={{0,18},{1,19},{2,16},{3,17},{4,22},{5,23},{6,20},{7,21},{8,26},{9,... | collective-permute-start | bytes 393224 | tf_op jit(solution)/shard_map/ppermute | solution.py:39
  101.7 1.8 %collective-permute-start.23 = (bf16[128,512]{1,0:T(8,128)(2,1)S(1)}, bf16[128,512]{1,0:T(8,128)(2,1)S(1)}, u32[]{:S(2)}, u32[]{:S(2)}) collective-permute-start(bf16[128,512]{1,0:T(8,128)(2,1)S(1)} %get-tuple-element.42), channel_id=1, source_target_pairs={{0,2},{1,3},{2,0},{3,1},{4,6},{5,7},{6,4},{7,5},{8,10},{9,11},{10,... | collective-permute-start | bytes 393224 | tf_op jit(solution)/shard_map/ppermute | solution.py:39
  104.0 2.6 %collective-permute-done.34.refs_12_ = bf16[128,512]{1,0:T(8,128)(2,1)S(1)} collective-permute-done((bf16[128,512]{1,0:T(8,128)(2,1)S(1)}, bf16[128,512]{1,0:T(8,128)(2,1)S(1)}, u32[]{:S(2)}, u32[]{:S(2)}) %collective-permute-start.34) | collective-permute-done | bytes 131104 | tf_op jit(solution)/shard_map/ppermute | solution.py:39
  106.6 2.2 %collective-permute-done.36.refs_14_ = bf16[128,512]{1,0:T(8,128)(2,1)S(1)} collective-permute-done((bf16[128,512]{1,0:T(8,128)(2,1)S(1)}, bf16[128,512]{1,0:T(8,128)(2,1)S(1)}, u32[]{:S(2)}, u32[]{:S(2)}) %collective-permute-start.36) | collective-permute-done | bytes 131104 | tf_op jit(solution)/shard_map/ppermute | solution.py:39
  111.9 2.6 %collective-permute-done.25.refs_7_ = bf16[128,512]{1,0:T(8,128)(2,1)S(1)} collective-permute-done((bf16[128,512]{1,0:T(8,128)(2,1)S(1)}, bf16[128,512]{1,0:T(8,128)(2,1)S(1)}, u32[]{:S(2)}, u32[]{:S(2)}) %collective-permute-start.25) | collective-permute-done | bytes 131104 | tf_op jit(solution)/shard_map/ppermute | solution.py:39
  114.5 3.0 %collective-permute-done.22.refs_4_ = bf16[128,512]{1,0:T(8,128)(2,1)S(1)} collective-permute-done((bf16[128,512]{1,0:T(8,128)(2,1)S(1)}, bf16[128,512]{1,0:T(8,128)(2,1)S(1)}, u32[]{:S(2)}, u32[]{:S(2)}) %collective-permute-start.22) | collective-permute-done | bytes 131104 | tf_op jit(solution)/shard_map/ppermute | solution.py:39
  117.5 2.6 %collective-permute-done.24.refs_6_ = bf16[128,512]{1,0:T(8,128)(2,1)S(1)} collective-permute-done((bf16[128,512]{1,0:T(8,128)(2,1)S(1)}, bf16[128,512]{1,0:T(8,128)(2,1)S(1)}, u32[]{:S(2)}, u32[]{:S(2)}) %collective-permute-start.24) | collective-permute-done | bytes 131104 | tf_op jit(solution)/shard_map/ppermute | solution.py:39
  (79 shorter events, 29.2 us)
Async XLA Ops:
  2.9 20.9 %collective-permute-start.10 = (bf16[72,1024]{1,0:T(8,128)(2,1)}, bf16[72,1024]{1,0:T(8,128)(2,1)S(1)}, u32[]{:S(2)}, u32[]{:S(2)}) collective-permute-start(bf16[72,1024]{1,0:T(8,128)(2,1)} %get-tuple-element.35), channel_id=1, source_target_pairs={{0,2},{1,3},{2,0},{3,1},{4,6},{5,7},{6,4},{7,5},{8,10},{9,11},{10,... | collective-permute-start | bytes 442376 | tf_op jit(solution)/shard_map/ppermute | solution.py:39
  5.9 18.0 %collective-permute-start.11 = (bf16[72,1024]{1,0:T(8,128)(2,1)}, bf16[72,1024]{1,0:T(8,128)(2,1)S(1)}, u32[]{:S(2)}, u32[]{:S(2)}) collective-permute-start(bf16[72,1024]{1,0:T(8,128)(2,1)} %get-tuple-element.36), channel_id=1, source_target_pairs={{0,3},{1,2},{2,1},{3,0},{4,7},{5,6},{6,5},{7,4},{8,11},{9,10},{10,... | collective-permute-start | bytes 442376 | tf_op jit(solution)/shard_map/ppermute | solution.py:39
  5.9 18.0 %collective-permute-start.9 = (bf16[72,1024]{1,0:T(8,128)(2,1)}, bf16[72,1024]{1,0:T(8,128)(2,1)S(1)}, u32[]{:S(2)}, u32[]{:S(2)}) collective-permute-start(bf16[72,1024]{1,0:T(8,128)(2,1)} %get-tuple-element.34), channel_id=1, source_target_pairs={{0,1},{1,0},{2,3},{3,2},{4,5},{5,4},{6,7},{7,6},{8,9},{9,8},{10,11... | collective-permute-start | bytes 442376 | tf_op jit(solution)/shard_map/ppermute | solution.py:39
  21.6 18.7 %collective-permute-start.2 = (bf16[128,1152]{1,0:T(8,128)(2,1)}, bf16[128,1152]{1,0:T(8,128)(2,1)S(1)}, u32[]{:S(2)}, u32[]{:S(2)}) collective-permute-start(bf16[128,1152]{1,0:T(8,128)(2,1)} %get-tuple-element.32), channel_id=1, source_target_pairs={{0,2},{2,4},{4,6},{6,8},{8,10},{10,12},{12,14},{14,0},{1,3},{3,5},... | collective-permute-start | bytes 884744 | tf_op jit(solution)/shard_map/ppermute | solution.py:592
  23.9 32.0 %collective-permute-start.12 = (bf16[288,1024]{1,0:T(8,128)(2,1)S(1)}, bf16[288,1024]{1,0:T(8,128)(2,1)S(1)}, u32[]{:S(2)}, u32[]{:S(2)}) collective-permute-start(bf16[288,1024]{1,0:T(8,128)(2,1)S(1)} %join.1.refs_4_), channel_id=1, source_target_pairs={{0,4},{2,6},{4,0},{6,2},{8,12},{10,14},{12,8},{14,10},{1,5},{3,7},... | collective-permute-start | bytes 1769480 | tf_op jit(solution)/shard_map/ppermute | solution.py:368
  25.6 31.1 %collective-permute-start.13 = (bf16[288,1024]{1,0:T(8,128)(2,1)S(1)}, bf16[288,1024]{1,0:T(8,128)(2,1)S(1)}, u32[]{:S(2)}, u32[]{:S(2)}) collective-permute-start(bf16[288,1024]{1,0:T(8,128)(2,1)S(1)} %join.1.refs_4_), channel_id=1, source_target_pairs={{0,0},{2,2},{4,8},{6,10},{8,4},{10,6},{12,12},{14,14},{1,1},{3,3},... | collective-permute-start | bytes 1769480 | tf_op jit(solution)/shard_map/ppermute | solution.py:368
  52.3 9.6 %collective-permute-start.26 = (bf16[128,1152]{1,0:T(8,128)(2,1)S(1)}, bf16[128,1152]{1,0:T(8,128)(2,1)S(1)}, u32[]{:S(2)}, u32[]{:S(2)}) collective-permute-start(bf16[128,1152]{1,0:T(8,128)(2,1)S(1)} %pad_maximum_fusion.refs_0_), channel_id=1, source_target_pairs={{0,16},{1,17},{2,18},{3,19},{4,20},{5,21},{6,22},{7,23},{8,24},{9,... | collective-permute-start | bytes 884744 | tf_op jit(solution)/shard_map/ppermute | solution.py:39
  53.9 13.3 %collective-permute-start.28 = (bf16[128,1152]{1,0:T(8,128)(2,1)S(1)}, bf16[128,1152]{1,0:T(8,128)(2,1)S(1)}, u32[]{:S(2)}, u32[]{:S(2)}) collective-permute-start(bf16[128,1152]{1,0:T(8,128)(2,1)S(1)} %pad_maximum_fusion.refs_0_), channel_id=1, source_target_pairs={{0,18},{1,19},{2,16},{3,17},{4,22},{5,23},{6,20},{7,21},{8,26},{9,... | collective-permute-start | bytes 884744 | tf_op jit(solution)/shard_map/ppermute | solution.py:39
  54.6 14.0 %collective-permute-start.7 = (bf16[128,1152]{1,0:T(8,128)(2,1)S(1)}, bf16[128,1152]{1,0:T(8,128)(2,1)S(1)}, u32[]{:S(2)}, u32[]{:S(2)}) collective-permute-start(bf16[128,1152]{1,0:T(8,128)(2,1)S(1)} %pad_maximum_fusion.refs_0_), channel_id=1, source_target_pairs={{0,2},{1,3},{2,0},{3,1},{4,6},{5,7},{6,4},{7,5},{8,10},{9,11},{10,... | collective-permute-start | bytes 884744 | tf_op jit(solution)/shard_map/ppermute | solution.py:39
  55.9 12.7 %collective-permute-start.18 = (bf16[288,512]{1,0:T(8,128)(2,1)S(1)}, bf16[288,512]{1,0:T(8,128)(2,1)S(1)}, u32[]{:S(2)}, u32[]{:S(2)}) collective-permute-start(bf16[288,512]{1,0:T(8,128)(2,1)S(1)} %get-tuple-element.53), channel_id=1, source_target_pairs={{0,0},{2,2},{4,8},{6,10},{8,4},{10,6},{12,12},{14,14},{1,1},{3,3},... | collective-permute-start | bytes 884744 | tf_op jit(solution)/shard_map/ppermute | solution.py:368
  56.7 14.1 %collective-permute-start.17 = (bf16[288,512]{1,0:T(8,128)(2,1)S(1)}, bf16[288,512]{1,0:T(8,128)(2,1)S(1)}, u32[]{:S(2)}, u32[]{:S(2)}) collective-permute-start(bf16[288,512]{1,0:T(8,128)(2,1)S(1)} %get-tuple-element.55), channel_id=1, source_target_pairs={{0,4},{2,6},{4,0},{6,2},{8,12},{10,14},{12,8},{14,10},{1,5},{3,7},... | collective-permute-start | bytes 884744 | tf_op jit(solution)/shard_map/ppermute | solution.py:368
  68.6 10.0 %collective-permute-start.19 = (bf16[288,512]{1,0:T(8,128)(2,1)S(1)}, bf16[288,512]{1,0:T(8,128)(2,1)S(1)}, u32[]{:S(2)}, u32[]{:S(2)}) collective-permute-start(bf16[288,512]{1,0:T(8,128)(2,1)S(1)} %collective-permute-done.18.refs_8_), channel_id=1, source_target_pairs={{0,4},{2,6},{4,0},{6,2},{8,12},{10,14},{12,8},{14,10},{1,5},{3,7},... | collective-permute-start | bytes 884744 | tf_op jit(solution)/shard_map/ppermute | solution.py:368
  70.8 10.9 %collective-permute-start.6 = (bf16[128,1152]{1,0:T(8,128)(2,1)S(1)}, bf16[128,1152]{1,0:T(8,128)(2,1)S(1)}, u32[]{:S(2)}, u32[]{:S(2)}) collective-permute-start(bf16[128,1152]{1,0:T(8,128)(2,1)S(1)} %pad_maximum_fusion.refs_0_), channel_id=1, source_target_pairs={{0,1},{1,0},{2,3},{3,2},{4,5},{5,4},{6,7},{7,6},{8,9},{9,8},{10,11... | collective-permute-start | bytes 884744 | tf_op jit(solution)/shard_map/ppermute | solution.py:39
  71.0 13.9 %collective-permute-start.14 = (bf16[288,512]{1,0:T(8,128)(2,1)S(1)}, bf16[288,512]{1,0:T(8,128)(2,1)S(1)}, u32[]{:S(2)}, u32[]{:S(2)}) collective-permute-start(bf16[288,512]{1,0:T(8,128)(2,1)S(1)} %get-tuple-element.56), channel_id=1, source_target_pairs={{0,4},{2,6},{4,0},{6,2},{8,12},{10,14},{12,8},{14,10},{1,5},{3,7},... | collective-permute-start | bytes 884744 | tf_op jit(solution)/shard_map/ppermute | solution.py:368
  72.7 18.4 %collective-permute-start.16 = (bf16[288,512]{1,0:T(8,128)(2,1)S(1)}, bf16[288,512]{1,0:T(8,128)(2,1)S(1)}, u32[]{:S(2)}, u32[]{:S(2)}) collective-permute-start(bf16[288,512]{1,0:T(8,128)(2,1)S(1)} %collective-permute-done.15.refs_8_), channel_id=1, source_target_pairs={{0,4},{2,6},{4,0},{6,2},{8,12},{10,14},{12,8},{14,10},{1,5},{3,7},... | collective-permute-start | bytes 884744 | tf_op jit(solution)/shard_map/ppermute | solution.py:368
  73.0 20.3 %collective-permute-start.8 = (bf16[128,1152]{1,0:T(8,128)(2,1)S(1)}, bf16[128,1152]{1,0:T(8,128)(2,1)S(1)}, u32[]{:S(2)}, u32[]{:S(2)}) collective-permute-start(bf16[128,1152]{1,0:T(8,128)(2,1)S(1)} %collective-permute-done.7.refs_2_), channel_id=1, source_target_pairs={{0,1},{1,0},{2,3},{3,2},{4,5},{5,4},{6,7},{7,6},{8,9},{9,8},{10,11... | collective-permute-start | bytes 884744 | tf_op jit(solution)/shard_map/ppermute | solution.py:39
  80.3 15.5 %collective-permute-start.31 = (bf16[128,512]{1,0:T(8,128)(2,1)S(1)}, bf16[128,512]{1,0:T(8,128)(2,1)S(1)}, u32[]{:S(2)}, u32[]{:S(2)}) collective-permute-start(bf16[128,512]{1,0:T(8,128)(2,1)S(1)} %get-tuple-element.46), channel_id=1, source_target_pairs={{0,16},{1,17},{2,18},{3,19},{4,20},{5,21},{6,22},{7,23},{8,24},{9,... | collective-permute-start | bytes 393224 | tf_op jit(solution)/shard_map/ppermute | solution.py:39
  81.6 15.4 %collective-permute-start.33 = (bf16[128,512]{1,0:T(8,128)(2,1)S(1)}, bf16[128,512]{1,0:T(8,128)(2,1)S(1)}, u32[]{:S(2)}, u32[]{:S(2)}) collective-permute-start(bf16[128,512]{1,0:T(8,128)(2,1)S(1)} %get-tuple-element.48), channel_id=1, source_target_pairs={{0,17},{1,16},{2,19},{3,18},{4,21},{5,20},{6,23},{7,22},{8,25},{9,... | collective-permute-start | bytes 393224 | tf_op jit(solution)/shard_map/ppermute | solution.py:39
  84.9 14.0 %collective-permute-start.35 = (bf16[128,512]{1,0:T(8,128)(2,1)S(1)}, bf16[128,512]{1,0:T(8,128)(2,1)S(1)}, u32[]{:S(2)}, u32[]{:S(2)}) collective-permute-start(bf16[128,512]{1,0:T(8,128)(2,1)S(1)} %get-tuple-element.50), channel_id=1, source_target_pairs={{0,18},{1,19},{2,16},{3,17},{4,22},{5,23},{6,20},{7,21},{8,26},{9,... | collective-permute-start | bytes 393224 | tf_op jit(solution)/shard_map/ppermute | solution.py:39
  97.0 9.6 %collective-permute-start.34 = (bf16[128,512]{1,0:T(8,128)(2,1)S(1)}, bf16[128,512]{1,0:T(8,128)(2,1)S(1)}, u32[]{:S(2)}, u32[]{:S(2)}) collective-permute-start(bf16[128,512]{1,0:T(8,128)(2,1)S(1)} %get-tuple-element.49), channel_id=1, source_target_pairs={{0,18},{1,19},{2,16},{3,17},{4,22},{5,23},{6,20},{7,21},{8,26},{9,... | collective-permute-start | bytes 393224 | tf_op jit(solution)/shard_map/ppermute | solution.py:39
  98.9 9.9 %collective-permute-start.36 = (bf16[128,512]{1,0:T(8,128)(2,1)S(1)}, bf16[128,512]{1,0:T(8,128)(2,1)S(1)}, u32[]{:S(2)}, u32[]{:S(2)}) collective-permute-start(bf16[128,512]{1,0:T(8,128)(2,1)S(1)} %get-tuple-element.51), channel_id=1, source_target_pairs={{0,19},{1,18},{2,17},{3,16},{4,23},{5,22},{6,21},{7,20},{8,27},{9,... | collective-permute-start | bytes 393224 | tf_op jit(solution)/shard_map/ppermute | solution.py:39
  101.7 10.2 %collective-permute-start.23 = (bf16[128,512]{1,0:T(8,128)(2,1)S(1)}, bf16[128,512]{1,0:T(8,128)(2,1)S(1)}, u32[]{:S(2)}, u32[]{:S(2)}) collective-permute-start(bf16[128,512]{1,0:T(8,128)(2,1)S(1)} %get-tuple-element.42), channel_id=1, source_target_pairs={{0,2},{1,3},{2,0},{3,1},{4,6},{5,7},{6,4},{7,5},{8,10},{9,11},{10,... | collective-permute-start | bytes 393224 | tf_op jit(solution)/shard_map/ppermute | solution.py:39
  103.5 11.0 %collective-permute-start.25 = (bf16[128,512]{1,0:T(8,128)(2,1)S(1)}, bf16[128,512]{1,0:T(8,128)(2,1)S(1)}, u32[]{:S(2)}, u32[]{:S(2)}) collective-permute-start(bf16[128,512]{1,0:T(8,128)(2,1)S(1)} %get-tuple-element.44), channel_id=1, source_target_pairs={{0,3},{1,2},{2,1},{3,0},{4,7},{5,6},{6,5},{7,4},{8,11},{9,10},{10,... | collective-permute-start | bytes 393224 | tf_op jit(solution)/shard_map/ppermute | solution.py:39
  109.1 11.1 %collective-permute-start.24 = (bf16[128,512]{1,0:T(8,128)(2,1)S(1)}, bf16[128,512]{1,0:T(8,128)(2,1)S(1)}, u32[]{:S(2)}, u32[]{:S(2)}) collective-permute-start(bf16[128,512]{1,0:T(8,128)(2,1)S(1)} %get-tuple-element.43), channel_id=1, source_target_pairs={{0,3},{1,2},{2,1},{3,0},{4,7},{5,6},{6,5},{7,4},{8,11},{9,10},{10,... | collective-permute-start | bytes 393224 | tf_op jit(solution)/shard_map/ppermute | solution.py:39
  (19 other events, 133.7 us)
where the time goes:
time: 122 us
  waiting for transfers between devices  40.6 us (33%)
  starting transfers between devices  39.2 us (32%)
  Pallas kernels  38.9 us (32%)
  local copies, waits for them, and re-layouts  2.56 us (2%)
    pallas_call x2, Pallas kernels, block_call(): pl.pallas_call(lambda *refs: block_kernel(frame, planes, first, refs), ou...  28.3 us
    ppermute x27, waiting for transfers between devices, shifted(): return lax.ppermute(value, AXES, pairs)  26.6 us
    ppermute x27, starting transfers between devices, shifted(): return lax.ppermute(value, AXES, pairs)  25.6 us
    ppermute x8, waiting for transfers between devices, spread_weight(): value = lax.ppermute(value, 'tm', whole)  14 us
    ppermute x8, starting transfers between devices, spread_weight(): value = lax.ppermute(value, 'tm', whole)  10.9 us
    pallas_call x4, Pallas kernels, project_call(): pl.pallas_call(lambda *refs: project_kernel(chunk, outer, inner, cores, *...  6.49 us
    unnamed x10, local copies, waits for them, and re-layouts  2.45 us
  transfers between devices with their start and end apart: 38, of which 13 were waited for; matrix products, arithmetic and copies ran while one was open for 0% of the time, Pallas kernels for 29%

commit v1 on v0

--- a/solution.py
+++ b/solution.py
@@ -245,12 +245,13 @@
 def cut_kernel(weight_ref, x_ref, *refs):
     _, _, inner, cores = axes_of()
     g, _, y, c = place_of()
-    head, tail, pieces, sem = refs[0], refs[1], refs[2:-1], refs[-1]
+    edges, pieces, sem = refs[: -1 - inner * cores], refs[-1 - inner * cores : -1], refs[-1]
     block = pieces[0].shape[1]
     near = x_ref.shape[1]
+    rows = [jnp.where(c == 0, near - 1, 0)] if cores == 2 else [0, near - 1]
     copies = [
-        pltpu.make_async_copy(x_ref.at[:, 0], head, sem.at[len(pieces)]),
-        pltpu.make_async_copy(x_ref.at[:, near - 1], tail, sem.at[len(pieces) + 1]),
+        pltpu.make_async_copy(x_ref.at[:, row], edge, sem.at[len(pieces) + n])
+        for n, (row, edge) in enumerate(zip(rows, edges))
     ]
     for n, (dy, dc) in enumerate(itertools.product(range(inner), range(cores))):
         to = (g * inner + lax.rem(y + dy, inner)) * cores + lax.rem(c + dc, cores)
@@ -278,18 +279,21 @@
     if depth % 8 or block % 128:
         to = [(g * inner + (y + dy) % inner) * cores + (c + dc) % cores for dy, dc in steps]
         pieces = [lax.dynamic_slice_in_dim(proj_weight, t * block, block, axis=1) for t in to]
-        return paired[:, 0], paired[:, -1], pieces
+        if cores == 2:
+            return [jnp.where(c == 0, paired[:, -1], paired[:, 0])], pieces
+        return [paired[:, 0], paired[:, -1]], pieces
     edge = jax.ShapeDtypeStruct(paired.shape[:1] + paired.shape[2:], paired.dtype)
-    head, tail, *pieces = pl.pallas_call(
+    sides = 1 if cores == 2 else 2
+    found = pl.pallas_call(
         cut_kernel,
-        out_shape=[edge, edge] + [jax.ShapeDtypeStruct((depth, block), proj_weight.dtype)] * len(steps),
+        out_shape=[edge] * sides + [jax.ShapeDtypeStruct((depth, block), proj_weight.dtype)] * len(steps),
         in_specs=[HBM, HBM],
-        out_specs=[VMEM] * (len(steps) + 2),
-        scratch_shapes=[pltpu.SemaphoreType.DMA((len(steps) + 2,))],
+        out_specs=[VMEM] * (len(steps) + sides),
+        scratch_shapes=[pltpu.SemaphoreType.DMA((len(steps) + sides,))],
         compiler_params=pltpu.CompilerParams(vmem_limit_bytes=60 << 20),
         name="cut",
     )(proj_weight, paired)
-    return head, tail, pieces
+    return found[:sides], found[sides:]
 
 
 def walk(outer):
@@ -579,9 +583,11 @@
     frames, height, across, channels = video_tokens.shape
     cores, along = lax.axis_size("rows"), lax.axis_size("tm")
     paired = video_tokens.reshape(frames, height // 2, 2, across, channels)
-    head, tail, pieces = cut(proj_weight, paired)
-    up = lax.ppermute(tail, "rows", [(i, (i + 1) % cores) for i in range(cores)])
-    down = lax.ppermute(head, "rows", [((i + 1) % cores, i) for i in range(cores)])
+    edges, pieces = cut(proj_weight, paired)
+    up = lax.ppermute(edges[-1], "rows", [(i, (i + 1) % cores) for i in range(cores)])
+    down = up
+    if len(edges) > 1:
+        down = lax.ppermute(edges[0], "rows", [((i + 1) % cores, i) for i in range(cores)])
     levels = spread_weight(pieces, frames // 2 * (height // 2) * (across // 2))
     shared = (paired, up, down, conv_weight, point_weight, depth_weight)
     sums, rims = [], []

time: 122 us -> 121 us (level)
    unnamed x10 -> x8, local copies, waits for them, and re-layouts: 2.45 us -> 1.78 us
  transfers between devices with their start and end apart: 38 -> 37, of which waited for: 13 -> 13; matrix products, arithmetic and copies ran while one was open for 0% -> 0% of each run, Pallas kernels for 29% -> 29%
where the time goes in v1:
time: 121 us; the launch traced here: 120 us
  waiting for transfers between devices  40.7 us (34%)
  Pallas kernels  38.8 us (32%)
  starting transfers between devices  38.6 us (32%)
  local copies, waits for them, and re-layouts  1.88 us (2%)
    pallas_call x2, Pallas kernels, block_call(): pl.pallas_call(lambda *refs: block_kernel(frame, planes, first, refs), ou...  28.3 us
    ppermute x27, waiting for transfers between devices, shifted(): return lax.ppermute(value, AXES, pairs)  26.7 us
    ppermute x27, starting transfers between devices, shifted(): return lax.ppermute(value, AXES, pairs)  25.6 us
    ppermute x8, waiting for transfers between devices, spread_weight(): value = lax.ppermute(value, 'tm', whole)  14 us
    ppermute x8, starting transfers between devices, spread_weight(): value = lax.ppermute(value, 'tm', whole)  10.7 us
    pallas_call x4, Pallas kernels, project_call(): pl.pallas_call(lambda *refs: project_kernel(chunk, outer, inner, cores, *...  6.48 us
  transfers between devices with their start and end apart: 37, of which 13 were waited for; matrix products, arithmetic and copies ran while one was open for 0% of the time, Pallas kernels for 29%

profile of v1, /device:TPU:0, one launch (start us, length us, event | category | flops | bytes accessed | tf_op | source)
XLA Modules:
  0.0 120.4 jit_solution(7294546844631768274)
XLA Ops:
  0.0 2.1 %cut.1 = (bf16[2,2,32,1152]{3,2,1,0:T(8,128)(2,1)}, bf16[72,1024]{1,0:T(8,128)(2,1)}, bf16[72,1024]{1,0:T(8,128)(2,1)}, bf16[72,1024]{1,0:T(8,128)(2,1)}, bf16[72,1024]{1,0:T(8,128)(2,1)}) custom-call(bf16[72,8192]{1,0:T(8,128)(2,1)} %weight_ref.1, bf16[2,8,2,32,1152]{4,3,2,1,0:T(8,128)(2,1)} %bitcast.3), custom_call_target="tpu_custom_call" | custom-call | tf_op jit(solution)/shard_map/cut/pallas_call | solution.py:287
  2.7 2.6 %collective-permute-start.10 = (bf16[72,1024]{1,0:T(8,128)(2,1)}, bf16[72,1024]{1,0:T(8,128)(2,1)S(1)}, u32[]{:S(2)}, u32[]{:S(2)}) collective-permute-start(bf16[72,1024]{1,0:T(8,128)(2,1)} %get-tuple-element.34), channel_id=1, source_target_pairs={{0,3},{1,2},{2,1},{3,0},{4,7},{5,6},{6,5},{7,4},{8,11},{9,10},{10,... | collective-permute-start | bytes 442376 | tf_op jit(solution)/shard_map/ppermute | solution.py:39
  6.5 14.2 %block_last.1 = (bf16[128,1152]{1,0:T(8,128)(2,1)}, f32[128,1152]{1,0:T(8,128)}) custom-call(bf16[2,8,2,32,1152]{4,3,2,1,0:T(8,128)(2,1)} %bitcast.4, bf16[2,2,32,1152]{3,2,1,0:T(8,128)(2,1)} %copy-done.2, bf16[2,2,32,1152]{3,2,1,0:T(8,128)(2,1)} %copy-done.2, bf16[3,3,9,128,128]{4,3,2,1,0:T(8,128)(2,1)} %refs_3_.3, bf16[1152,1152]{1,0:T(8,128)(2,1)} %refs_4_.3, ...), custom_call_target="tpu_custom_call" | custom-call | tf_op jit(solution)/shard_map/block_last/pallas_call | solution.py:211
  20.7 1.8 %collective-permute-start.1 = (bf16[128,1152]{1,0:T(8,128)(2,1)}, bf16[128,1152]{1,0:T(8,128)(2,1)S(1)}, u32[]{:S(2)}, u32[]{:S(2)}) collective-permute-start(bf16[128,1152]{1,0:T(8,128)(2,1)} %get-tuple-element.30), channel_id=1, source_target_pairs={{0,2},{2,4},{4,6},{6,8},{8,10},{10,12},{12,14},{14,0},{1,3},{3,5},... | collective-permute-start | bytes 884744 | tf_op jit(solution)/shard_map/ppermute | solution.py:598
  22.7 1.6 %collective-permute-start.11 = (bf16[288,1024]{1,0:T(8,128)(2,1)S(1)}, bf16[288,1024]{1,0:T(8,128)(2,1)S(1)}, u32[]{:S(2)}, u32[]{:S(2)}) collective-permute-start(bf16[288,1024]{1,0:T(8,128)(2,1)S(1)} %join.1.refs_4_), channel_id=1, source_target_pairs={{0,4},{2,6},{4,0},{6,2},{8,12},{10,14},{12,8},{14,10},{1,5},{3,7},... | collective-permute-start | bytes 1769480 | tf_op jit(solution)/shard_map/ppermute | solution.py:372
  25.0 14.1 %block_first.1.refs_0_ = f32[128,1152]{1,0:T(8,128)} custom-call(bf16[2,8,2,32,1152]{4,3,2,1,0:T(8,128)(2,1)} %bitcast.5, bf16[2,2,32,1152]{3,2,1,0:T(8,128)(2,1)} %copy-done.2, bf16[2,2,32,1152]{3,2,1,0:T(8,128)(2,1)} %copy-done.2, bf16[3,3,9,128,128]{4,3,2,1,0:T(8,128)(2,1)} %refs_3_.3, bf16[1152,1152]{1,0:T(8,128)(2,1)} %refs_4_.3, ...), custom_call_target="tpu_custom_call" | custom-call | tf_op jit(solution)/shard_map/block_first/pallas_call | solution.py:211
  40.5 4.4 %collective-permute-start.2 = (bf16[32,1152]{1,0:T(8,128)(2,1)S(1)}, bf16[32,1152]{1,0:T(8,128)(2,1)S(1)}, u32[]{:S(2)}, u32[]{:S(2)}) collective-permute-start(bf16[32,1152]{1,0:T(8,128)(2,1)S(1)} %get-tuple-element.58), channel_id=1, source_target_pairs={{0,4},{1,5},{2,6},{3,7},{4,8},{5,9},{6,10},{7,11},{8,12},{9,13},{1... | collective-permute-start | bytes 221192 | tf_op jit(solution)/shard_map/ppermute | solution.py:39
  45.0 2.4 %collective-permute-start.4 = (bf16[32,1152]{1,0:T(8,128)(2,1)S(1)}, bf16[32,1152]{1,0:T(8,128)(2,1)S(1)}, u32[]{:S(2)}, u32[]{:S(2)}) collective-permute-start(bf16[32,1152]{1,0:T(8,128)(2,1)S(1)} %get-tuple-element.56), channel_id=1, source_target_pairs={{0,12},{1,13},{2,14},{3,15},{4,0},{5,1},{6,2},{7,3},{8,4},{9,5},{1... | collective-permute-start | bytes 221192 | tf_op jit(solution)/shard_map/ppermute | solution.py:39
  47.4 3.8 %collective-permute-done.3 = bf16[32,1152]{1,0:T(8,128)(2,1)S(1)} collective-permute-done((bf16[32,1152]{1,0:T(8,128)(2,1)S(1)}, bf16[32,1152]{1,0:T(8,128)(2,1)S(1)}, u32[]{:S(2)}, u32[]{:S(2)}) %collective-permute-start.3) | collective-permute-done | bytes 73760 | tf_op jit(solution)/shard_map/ppermute | solution.py:39
  55.6 2.9 %collective-permute-start.16 = (bf16[288,512]{1,0:T(8,128)(2,1)S(1)}, bf16[288,512]{1,0:T(8,128)(2,1)S(1)}, u32[]{:S(2)}, u32[]{:S(2)}) collective-permute-start(bf16[288,512]{1,0:T(8,128)(2,1)S(1)} %get-tuple-element.53), channel_id=1, source_target_pairs={{0,4},{2,6},{4,0},{6,2},{8,12},{10,14},{12,8},{14,10},{1,5},{3,7},... | collective-permute-start | bytes 884744 | tf_op jit(solution)/shard_map/ppermute | solution.py:372
  58.5 2.4 %collective-permute-done.25.refs_0_ = bf16[128,1152]{1,0:T(8,128)(2,1)S(1)} collective-permute-done((bf16[128,1152]{1,0:T(8,128)(2,1)S(1)}, bf16[128,1152]{1,0:T(8,128)(2,1)S(1)}, u32[]{:S(2)}, u32[]{:S(2)}) %collective-permute-start.25) | collective-permute-done | bytes 294944 | tf_op jit(solution)/shard_map/ppermute | solution.py:39
  61.6 4.4 %collective-permute-done.27.refs_2_ = bf16[128,1152]{1,0:T(8,128)(2,1)S(1)} collective-permute-done((bf16[128,1152]{1,0:T(8,128)(2,1)S(1)}, bf16[128,1152]{1,0:T(8,128)(2,1)S(1)}, u32[]{:S(2)}, u32[]{:S(2)}) %collective-permute-start.27) | collective-permute-done | bytes 294944 | tf_op jit(solution)/shard_map/ppermute | solution.py:39
  67.4 2.1 %collective-permute-start.18 = (bf16[288,512]{1,0:T(8,128)(2,1)S(1)}, bf16[288,512]{1,0:T(8,128)(2,1)S(1)}, u32[]{:S(2)}, u32[]{:S(2)}) collective-permute-start(bf16[288,512]{1,0:T(8,128)(2,1)S(1)} %collective-permute-done.17.refs_8_), channel_id=1, source_target_pairs={{0,4},{2,6},{4,0},{6,2},{8,12},{10,14},{12,8},{14,10},{1,5},{3,7},... | collective-permute-start | bytes 884744 | tf_op jit(solution)/shard_map/ppermute | solution.py:372
  69.8 1.7 %collective-permute-start.13 = (bf16[288,512]{1,0:T(8,128)(2,1)S(1)}, bf16[288,512]{1,0:T(8,128)(2,1)S(1)}, u32[]{:S(2)}, u32[]{:S(2)}) collective-permute-start(bf16[288,512]{1,0:T(8,128)(2,1)S(1)} %get-tuple-element.54), channel_id=1, source_target_pairs={{0,4},{2,6},{4,0},{6,2},{8,12},{10,14},{12,8},{14,10},{1,5},{3,7},... | collective-permute-start | bytes 884744 | tf_op jit(solution)/shard_map/ppermute | solution.py:372
  71.8 5.6 %collective-permute-done.18.refs_9_ = bf16[288,512]{1,0:T(8,128)(2,1)S(1)} collective-permute-done((bf16[288,512]{1,0:T(8,128)(2,1)S(1)}, bf16[288,512]{1,0:T(8,128)(2,1)S(1)}, u32[]{:S(2)}, u32[]{:S(2)}) %collective-permute-start.18) | collective-permute-done | bytes 294944 | tf_op jit(solution)/shard_map/ppermute | solution.py:372
  80.4 3.3 %collective-permute-done.13.refs_7_ = bf16[288,512]{1,0:T(8,128)(2,1)S(1)} collective-permute-done((bf16[288,512]{1,0:T(8,128)(2,1)S(1)}, bf16[288,512]{1,0:T(8,128)(2,1)S(1)}, u32[]{:S(2)}, u32[]{:S(2)}) %collective-permute-start.13) | collective-permute-done | bytes 294944 | tf_op jit(solution)/shard_map/ppermute | solution.py:372
  84.7 5.1 %collective-permute-done.15.refs_9_ = bf16[288,512]{1,0:T(8,128)(2,1)S(1)} collective-permute-done((bf16[288,512]{1,0:T(8,128)(2,1)S(1)}, bf16[288,512]{1,0:T(8,128)(2,1)S(1)}, u32[]{:S(2)}, u32[]{:S(2)}) %collective-permute-start.15) | collective-permute-done | bytes 294944 | tf_op jit(solution)/shard_map/ppermute | solution.py:372
  95.8 1.9 %collective-permute-start.33 = (bf16[128,512]{1,0:T(8,128)(2,1)S(1)}, bf16[128,512]{1,0:T(8,128)(2,1)S(1)}, u32[]{:S(2)}, u32[]{:S(2)}) collective-permute-start(bf16[128,512]{1,0:T(8,128)(2,1)S(1)} %get-tuple-element.47), channel_id=1, source_target_pairs={{0,18},{1,19},{2,16},{3,17},{4,22},{5,23},{6,20},{7,21},{8,26},{9,... | collective-permute-start | bytes 393224 | tf_op jit(solution)/shard_map/ppermute | solution.py:39
  100.5 1.8 %collective-permute-start.22 = (bf16[128,512]{1,0:T(8,128)(2,1)S(1)}, bf16[128,512]{1,0:T(8,128)(2,1)S(1)}, u32[]{:S(2)}, u32[]{:S(2)}) collective-permute-start(bf16[128,512]{1,0:T(8,128)(2,1)S(1)} %get-tuple-element.40), channel_id=1, source_target_pairs={{0,2},{1,3},{2,0},{3,1},{4,6},{5,7},{6,4},{7,5},{8,10},{9,11},{10,... | collective-permute-start | bytes 393224 | tf_op jit(solution)/shard_map/ppermute | solution.py:39
  102.8 2.6 %collective-permute-done.33.refs_12_ = bf16[128,512]{1,0:T(8,128)(2,1)S(1)} collective-permute-done((bf16[128,512]{1,0:T(8,128)(2,1)S(1)}, bf16[128,512]{1,0:T(8,128)(2,1)S(1)}, u32[]{:S(2)}, u32[]{:S(2)}) %collective-permute-start.33) | collective-permute-done | bytes 131104 | tf_op jit(solution)/shard_map/ppermute | solution.py:39
  105.4 2.2 %collective-permute-done.35.refs_14_ = bf16[128,512]{1,0:T(8,128)(2,1)S(1)} collective-permute-done((bf16[128,512]{1,0:T(8,128)(2,1)S(1)}, bf16[128,512]{1,0:T(8,128)(2,1)S(1)}, u32[]{:S(2)}, u32[]{:S(2)}) %collective-permute-start.35) | collective-permute-done | bytes 131104 | tf_op jit(solution)/shard_map/ppermute | solution.py:39
  110.7 2.6 %collective-permute-done.24.refs_7_ = bf16[128,512]{1,0:T(8,128)(2,1)S(1)} collective-permute-done((bf16[128,512]{1,0:T(8,128)(2,1)S(1)}, bf16[128,512]{1,0:T(8,128)(2,1)S(1)}, u32[]{:S(2)}, u32[]{:S(2)}) %collective-permute-start.24) | collective-permute-done | bytes 131104 | tf_op jit(solution)/shard_map/ppermute | solution.py:39
  113.3 3.0 %collective-permute-done.21.refs_4_ = bf16[128,512]{1,0:T(8,128)(2,1)S(1)} collective-permute-done((bf16[128,512]{1,0:T(8,128)(2,1)S(1)}, bf16[128,512]{1,0:T(8,128)(2,1)S(1)}, u32[]{:S(2)}, u32[]{:S(2)}) %collective-permute-start.21) | collective-permute-done | bytes 131104 | tf_op jit(solution)/shard_map/ppermute | solution.py:39
  116.3 2.6 %collective-permute-done.23.refs_6_ = bf16[128,512]{1,0:T(8,128)(2,1)S(1)} collective-permute-done((bf16[128,512]{1,0:T(8,128)(2,1)S(1)}, bf16[128,512]{1,0:T(8,128)(2,1)S(1)}, u32[]{:S(2)}, u32[]{:S(2)}) %collective-permute-start.23) | collective-permute-done | bytes 131104 | tf_op jit(solution)/shard_map/ppermute | solution.py:39
  (75 shorter events, 28.7 us)
Async XLA Ops:
  2.7 19.9 %collective-permute-start.10 = (bf16[72,1024]{1,0:T(8,128)(2,1)}, bf16[72,1024]{1,0:T(8,128)(2,1)S(1)}, u32[]{:S(2)}, u32[]{:S(2)}) collective-permute-start(bf16[72,1024]{1,0:T(8,128)(2,1)} %get-tuple-element.34), channel_id=1, source_target_pairs={{0,3},{1,2},{2,1},{3,0},{4,7},{5,6},{6,5},{7,4},{8,11},{9,10},{10,... | collective-permute-start | bytes 442376 | tf_op jit(solution)/shard_map/ppermute | solution.py:39
  5.3 17.2 %collective-permute-start.8 = (bf16[72,1024]{1,0:T(8,128)(2,1)}, bf16[72,1024]{1,0:T(8,128)(2,1)S(1)}, u32[]{:S(2)}, u32[]{:S(2)}) collective-permute-start(bf16[72,1024]{1,0:T(8,128)(2,1)} %get-tuple-element.32), channel_id=1, source_target_pairs={{0,1},{1,0},{2,3},{3,2},{4,5},{5,4},{6,7},{7,6},{8,9},{9,8},{10,11... | collective-permute-start | bytes 442376 | tf_op jit(solution)/shard_map/ppermute | solution.py:39
  5.4 17.2 %collective-permute-start.9 = (bf16[72,1024]{1,0:T(8,128)(2,1)}, bf16[72,1024]{1,0:T(8,128)(2,1)S(1)}, u32[]{:S(2)}, u32[]{:S(2)}) collective-permute-start(bf16[72,1024]{1,0:T(8,128)(2,1)} %get-tuple-element.33), channel_id=1, source_target_pairs={{0,2},{1,3},{2,0},{3,1},{4,6},{5,7},{6,4},{7,5},{8,10},{9,11},{10,... | collective-permute-start | bytes 442376 | tf_op jit(solution)/shard_map/ppermute | solution.py:39
  20.7 18.4 %collective-permute-start.1 = (bf16[128,1152]{1,0:T(8,128)(2,1)}, bf16[128,1152]{1,0:T(8,128)(2,1)S(1)}, u32[]{:S(2)}, u32[]{:S(2)}) collective-permute-start(bf16[128,1152]{1,0:T(8,128)(2,1)} %get-tuple-element.30), channel_id=1, source_target_pairs={{0,2},{2,4},{4,6},{6,8},{8,10},{10,12},{12,14},{14,0},{1,3},{3,5},... | collective-permute-start | bytes 884744 | tf_op jit(solution)/shard_map/ppermute | solution.py:598
  22.7 32.2 %collective-permute-start.11 = (bf16[288,1024]{1,0:T(8,128)(2,1)S(1)}, bf16[288,1024]{1,0:T(8,128)(2,1)S(1)}, u32[]{:S(2)}, u32[]{:S(2)}) collective-permute-start(bf16[288,1024]{1,0:T(8,128)(2,1)S(1)} %join.1.refs_4_), channel_id=1, source_target_pairs={{0,4},{2,6},{4,0},{6,2},{8,12},{10,14},{12,8},{14,10},{1,5},{3,7},... | collective-permute-start | bytes 1769480 | tf_op jit(solution)/shard_map/ppermute | solution.py:372
  24.3 31.3 %collective-permute-start.12 = (bf16[288,1024]{1,0:T(8,128)(2,1)S(1)}, bf16[288,1024]{1,0:T(8,128)(2,1)S(1)}, u32[]{:S(2)}, u32[]{:S(2)}) collective-permute-start(bf16[288,1024]{1,0:T(8,128)(2,1)S(1)} %join.1.refs_4_), channel_id=1, source_target_pairs={{0,0},{2,2},{4,8},{6,10},{8,4},{10,6},{12,12},{14,14},{1,1},{3,3},... | collective-permute-start | bytes 1769480 | tf_op jit(solution)/shard_map/ppermute | solution.py:372
  51.3 9.6 %collective-permute-start.25 = (bf16[128,1152]{1,0:T(8,128)(2,1)S(1)}, bf16[128,1152]{1,0:T(8,128)(2,1)S(1)}, u32[]{:S(2)}, u32[]{:S(2)}) collective-permute-start(bf16[128,1152]{1,0:T(8,128)(2,1)S(1)} %pad_maximum_fusion.refs_0_), channel_id=1, source_target_pairs={{0,16},{1,17},{2,18},{3,19},{4,20},{5,21},{6,22},{7,23},{8,24},{9,... | collective-permute-start | bytes 884744 | tf_op jit(solution)/shard_map/ppermute | solution.py:39
  52.8 13.2 %collective-permute-start.27 = (bf16[128,1152]{1,0:T(8,128)(2,1)S(1)}, bf16[128,1152]{1,0:T(8,128)(2,1)S(1)}, u32[]{:S(2)}, u32[]{:S(2)}) collective-permute-start(bf16[128,1152]{1,0:T(8,128)(2,1)S(1)} %pad_maximum_fusion.refs_0_), channel_id=1, source_target_pairs={{0,18},{1,19},{2,16},{3,17},{4,22},{5,23},{6,20},{7,21},{8,26},{9,... | collective-permute-start | bytes 884744 | tf_op jit(solution)/shard_map/ppermute | solution.py:39
  53.4 14.0 %collective-permute-start.6 = (bf16[128,1152]{1,0:T(8,128)(2,1)S(1)}, bf16[128,1152]{1,0:T(8,128)(2,1)S(1)}, u32[]{:S(2)}, u32[]{:S(2)}) collective-permute-start(bf16[128,1152]{1,0:T(8,128)(2,1)S(1)} %pad_maximum_fusion.refs_0_), channel_id=1, source_target_pairs={{0,2},{1,3},{2,0},{3,1},{4,6},{5,7},{6,4},{7,5},{8,10},{9,11},{10,... | collective-permute-start | bytes 884744 | tf_op jit(solution)/shard_map/ppermute | solution.py:39
  54.9 12.5 %collective-permute-start.17 = (bf16[288,512]{1,0:T(8,128)(2,1)S(1)}, bf16[288,512]{1,0:T(8,128)(2,1)S(1)}, u32[]{:S(2)}, u32[]{:S(2)}) collective-permute-start(bf16[288,512]{1,0:T(8,128)(2,1)S(1)} %get-tuple-element.51), channel_id=1, source_target_pairs={{0,0},{2,2},{4,8},{6,10},{8,4},{10,6},{12,12},{14,14},{1,1},{3,3},... | collective-permute-start | bytes 884744 | tf_op jit(solution)/shard_map/ppermute | solution.py:372
  55.6 13.9 %collective-permute-start.16 = (bf16[288,512]{1,0:T(8,128)(2,1)S(1)}, bf16[288,512]{1,0:T(8,128)(2,1)S(1)}, u32[]{:S(2)}, u32[]{:S(2)}) collective-permute-start(bf16[288,512]{1,0:T(8,128)(2,1)S(1)} %get-tuple-element.53), channel_id=1, source_target_pairs={{0,4},{2,6},{4,0},{6,2},{8,12},{10,14},{12,8},{14,10},{1,5},{3,7},... | collective-permute-start | bytes 884744 | tf_op jit(solution)/shard_map/ppermute | solution.py:372
  67.4 10.0 %collective-permute-start.18 = (bf16[288,512]{1,0:T(8,128)(2,1)S(1)}, bf16[288,512]{1,0:T(8,128)(2,1)S(1)}, u32[]{:S(2)}, u32[]{:S(2)}) collective-permute-start(bf16[288,512]{1,0:T(8,128)(2,1)S(1)} %collective-permute-done.17.refs_8_), channel_id=1, source_target_pairs={{0,4},{2,6},{4,0},{6,2},{8,12},{10,14},{12,8},{14,10},{1,5},{3,7},... | collective-permute-start | bytes 884744 | tf_op jit(solution)/shard_map/ppermute | solution.py:372
  69.5 10.9 %collective-permute-start.5 = (bf16[128,1152]{1,0:T(8,128)(2,1)S(1)}, bf16[128,1152]{1,0:T(8,128)(2,1)S(1)}, u32[]{:S(2)}, u32[]{:S(2)}) collective-permute-start(bf16[128,1152]{1,0:T(8,128)(2,1)S(1)} %pad_maximum_fusion.refs_0_), channel_id=1, source_target_pairs={{0,1},{1,0},{2,3},{3,2},{4,5},{5,4},{6,7},{7,6},{8,9},{9,8},{10,11... | collective-permute-start | bytes 884744 | tf_op jit(solution)/shard_map/ppermute | solution.py:39
  69.8 13.9 %collective-permute-start.13 = (bf16[288,512]{1,0:T(8,128)(2,1)S(1)}, bf16[288,512]{1,0:T(8,128)(2,1)S(1)}, u32[]{:S(2)}, u32[]{:S(2)}) collective-permute-start(bf16[288,512]{1,0:T(8,128)(2,1)S(1)} %get-tuple-element.54), channel_id=1, source_target_pairs={{0,4},{2,6},{4,0},{6,2},{8,12},{10,14},{12,8},{14,10},{1,5},{3,7},... | collective-permute-start | bytes 884744 | tf_op jit(solution)/shard_map/ppermute | solution.py:372
  71.5 18.4 %collective-permute-start.15 = (bf16[288,512]{1,0:T(8,128)(2,1)S(1)}, bf16[288,512]{1,0:T(8,128)(2,1)S(1)}, u32[]{:S(2)}, u32[]{:S(2)}) collective-permute-start(bf16[288,512]{1,0:T(8,128)(2,1)S(1)} %collective-permute-done.14.refs_8_), channel_id=1, source_target_pairs={{0,4},{2,6},{4,0},{6,2},{8,12},{10,14},{12,8},{14,10},{1,5},{3,7},... | collective-permute-start | bytes 884744 | tf_op jit(solution)/shard_map/ppermute | solution.py:372
  71.8 20.3 %collective-permute-start.7 = (bf16[128,1152]{1,0:T(8,128)(2,1)S(1)}, bf16[128,1152]{1,0:T(8,128)(2,1)S(1)}, u32[]{:S(2)}, u32[]{:S(2)}) collective-permute-start(bf16[128,1152]{1,0:T(8,128)(2,1)S(1)} %collective-permute-done.6.refs_2_), channel_id=1, source_target_pairs={{0,1},{1,0},{2,3},{3,2},{4,5},{5,4},{6,7},{7,6},{8,9},{9,8},{10,11... | collective-permute-start | bytes 884744 | tf_op jit(solution)/shard_map/ppermute | solution.py:39
  79.0 15.5 %collective-permute-start.30 = (bf16[128,512]{1,0:T(8,128)(2,1)S(1)}, bf16[128,512]{1,0:T(8,128)(2,1)S(1)}, u32[]{:S(2)}, u32[]{:S(2)}) collective-permute-start(bf16[128,512]{1,0:T(8,128)(2,1)S(1)} %get-tuple-element.44), channel_id=1, source_target_pairs={{0,16},{1,17},{2,18},{3,19},{4,20},{5,21},{6,22},{7,23},{8,24},{9,... | collective-permute-start | bytes 393224 | tf_op jit(solution)/shard_map/ppermute | solution.py:39
  80.4 15.4 %collective-permute-start.32 = (bf16[128,512]{1,0:T(8,128)(2,1)S(1)}, bf16[128,512]{1,0:T(8,128)(2,1)S(1)}, u32[]{:S(2)}, u32[]{:S(2)}) collective-permute-start(bf16[128,512]{1,0:T(8,128)(2,1)S(1)} %get-tuple-element.46), channel_id=1, source_target_pairs={{0,17},{1,16},{2,19},{3,18},{4,21},{5,20},{6,23},{7,22},{8,25},{9,... | collective-permute-start | bytes 393224 | tf_op jit(solution)/shard_map/ppermute | solution.py:39
  83.7 14.0 %collective-permute-start.34 = (bf16[128,512]{1,0:T(8,128)(2,1)S(1)}, bf16[128,512]{1,0:T(8,128)(2,1)S(1)}, u32[]{:S(2)}, u32[]{:S(2)}) collective-permute-start(bf16[128,512]{1,0:T(8,128)(2,1)S(1)} %get-tuple-element.48), channel_id=1, source_target_pairs={{0,18},{1,19},{2,16},{3,17},{4,22},{5,23},{6,20},{7,21},{8,26},{9,... | collective-permute-start | bytes 393224 | tf_op jit(solution)/shard_map/ppermute | solution.py:39
  95.8 9.6 %collective-permute-start.33 = (bf16[128,512]{1,0:T(8,128)(2,1)S(1)}, bf16[128,512]{1,0:T(8,128)(2,1)S(1)}, u32[]{:S(2)}, u32[]{:S(2)}) collective-permute-start(bf16[128,512]{1,0:T(8,128)(2,1)S(1)} %get-tuple-element.47), channel_id=1, source_target_pairs={{0,18},{1,19},{2,16},{3,17},{4,22},{5,23},{6,20},{7,21},{8,26},{9,... | collective-permute-start | bytes 393224 | tf_op jit(solution)/shard_map/ppermute | solution.py:39
  97.7 9.9 %collective-permute-start.35 = (bf16[128,512]{1,0:T(8,128)(2,1)S(1)}, bf16[128,512]{1,0:T(8,128)(2,1)S(1)}, u32[]{:S(2)}, u32[]{:S(2)}) collective-permute-start(bf16[128,512]{1,0:T(8,128)(2,1)S(1)} %get-tuple-element.49), channel_id=1, source_target_pairs={{0,19},{1,18},{2,17},{3,16},{4,23},{5,22},{6,21},{7,20},{8,27},{9,... | collective-permute-start | bytes 393224 | tf_op jit(solution)/shard_map/ppermute | solution.py:39
  100.5 10.2 %collective-permute-start.22 = (bf16[128,512]{1,0:T(8,128)(2,1)S(1)}, bf16[128,512]{1,0:T(8,128)(2,1)S(1)}, u32[]{:S(2)}, u32[]{:S(2)}) collective-permute-start(bf16[128,512]{1,0:T(8,128)(2,1)S(1)} %get-tuple-element.40), channel_id=1, source_target_pairs={{0,2},{1,3},{2,0},{3,1},{4,6},{5,7},{6,4},{7,5},{8,10},{9,11},{10,... | collective-permute-start | bytes 393224 | tf_op jit(solution)/shard_map/ppermute | solution.py:39
  102.3 11.0 %collective-permute-start.24 = (bf16[128,512]{1,0:T(8,128)(2,1)S(1)}, bf16[128,512]{1,0:T(8,128)(2,1)S(1)}, u32[]{:S(2)}, u32[]{:S(2)}) collective-permute-start(bf16[128,512]{1,0:T(8,128)(2,1)S(1)} %get-tuple-element.42), channel_id=1, source_target_pairs={{0,3},{1,2},{2,1},{3,0},{4,7},{5,6},{6,5},{7,4},{8,11},{9,10},{10,... | collective-permute-start | bytes 393224 | tf_op jit(solution)/shard_map/ppermute | solution.py:39
  107.8 11.1 %collective-permute-start.23 = (bf16[128,512]{1,0:T(8,128)(2,1)S(1)}, bf16[128,512]{1,0:T(8,128)(2,1)S(1)}, u32[]{:S(2)}, u32[]{:S(2)}) collective-permute-start(bf16[128,512]{1,0:T(8,128)(2,1)S(1)} %get-tuple-element.41), channel_id=1, source_target_pairs={{0,3},{1,2},{2,1},{3,0},{4,7},{5,6},{6,5},{7,4},{8,11},{9,10},{10,... | collective-permute-start | bytes 393224 | tf_op jit(solution)/shard_map/ppermute | solution.py:39
  (17 other events, 127.9 us)

commit v2 on v1

--- a/solution.py
+++ b/solution.py
@@ -481,15 +481,14 @@
     ]
 
 
-def collect_kernel(*refs):
+def collect_kernel(h, chunks, *refs):
     groups, _, inner, cores = axes_of()
     g, _, y, c = place_of()
-    pieces, out_ref, sem = refs[:-2], refs[-2], refs[-1]
+    pieces, out_ref, sem = refs[: groups * inner * cores], refs[-2], refs[-1]
     block = pieces[0].shape[1]
-    chunks = len(pieces) // (groups * inner * cores)
     copies = []
-    where = itertools.product(range(groups), range(inner), range(cores), range(chunks))
-    for n, (dg, dy, dc, h) in enumerate(where):
+    where = itertools.product(range(groups), range(inner), range(cores))
+    for n, (dg, dy, dc) in enumerate(where):
         source = lax.rem(g + groups - dg, groups) * inner + lax.rem(y + inner - dy, inner)
         source = source * cores + lax.rem(c + cores - dc, cores)
         lanes = pl.ds(pl.multiple_of((source * chunks + h) * block, 128), block)
@@ -522,16 +521,22 @@
             for (dy, dc), piece in zip(steps, pieces):
                 arrived[dg, dy, dc, h] = shifted(piece, (dg, 0, dy, dc))
     if fits:
-        pieces = [piece for _, piece in sorted(arrived.items())]
-        return pl.pallas_call(
-            collect_kernel,
-            out_shape=jax.ShapeDtypeStruct((count, len(pieces) // len(levels) * block), jnp.bfloat16),
-            in_specs=[VMEM] * len(pieces),
-            out_specs=HBM,
-            scratch_shapes=[pltpu.SemaphoreType.DMA((len(pieces),))],
-            compiler_params=pltpu.CompilerParams(vmem_limit_bytes=8 << 20),
-            name="collect",
-        )(*pieces)
+        out = ()
+        for h in range(len(levels)):
+            pieces = [piece for key, piece in sorted(arrived.items()) if key[3] == h]
+            out = (
+                pl.pallas_call(
+                    lambda *refs, h=h: collect_kernel(h, len(levels), *refs),
+                    out_shape=jax.ShapeDtypeStruct((count, len(pieces) * block), jnp.bfloat16),
+                    in_specs=[VMEM] * len(pieces) + [HBM] * len(out),
+                    out_specs=HBM,
+                    scratch_shapes=[pltpu.SemaphoreType.DMA((len(pieces),))],
+                    input_output_aliases={len(pieces): 0} if out else {},
+                    compiler_params=pltpu.CompilerParams(vmem_limit_bytes=8 << 20),
+                    name="collect",
+                )(*pieces, *out),
+            )
+        return out[0]
     out = jnp.zeros((count, groups * inner * cores * block), jnp.bfloat16)
     for (dg, dy, dc, _), piece in sorted(arrived.items()):
         source = (((g - dg) % groups) * inner + (y - dy) % inner) * cores + (c - dc) % cores

time: 121 us -> 127 us (1.050)
  starting transfers between devices: 38.6 us -> 54.5 us
  waiting for transfers between devices: 40.7 us -> 30.6 us
    ppermute x8, starting transfers between devices: 10.7 us -> 24 us  [spread_weight(): value = lax.ppermute(value, 'tm', whole)]
    ppermute x27, waiting for transfers between devices: 26.7 us -> 20.3 us  [shifted(): return lax.ppermute(value, AXES, pairs)]
    ppermute x8, waiting for transfers between devices: 14 us -> 10.3 us  [spread_weight(): value = lax.ppermute(value, 'tm', whole)]
    ppermute x27, starting transfers between devices: 25.6 us -> 28.5 us  [shifted(): return lax.ppermute(value, AXES, pairs)]
  transfers between devices with their start and end apart: 37 -> 37, of which waited for: 13 -> 9; matrix products, arithmetic and copies ran while one was open for 0% -> 0% of each run, Pallas kernels for 29% -> 29%
where the time goes in v2:
time: 127 us
  starting transfers between devices  54.5 us (43%)
  Pallas kernels  39.3 us (31%)
  waiting for transfers between devices  30.6 us (24%)
  local copies, waits for them, and re-layouts  1.88 us (1%)
    ppermute x27, starting transfers between devices, shifted(): return lax.ppermute(value, AXES, pairs)  28.5 us
    pallas_call x2, Pallas kernels, block_call(): pl.pallas_call(lambda *refs: block_kernel(frame, planes, first, refs), ou...  28.3 us
    ppermute x8, starting transfers between devices, spread_weight(): value = lax.ppermute(value, 'tm', whole)  24 us
    ppermute x27, waiting for transfers between devices, shifted(): return lax.ppermute(value, AXES, pairs)  20.3 us
    ppermute x8, waiting for transfers between devices, spread_weight(): value = lax.ppermute(value, 'tm', whole)  10.3 us
    pallas_call x4, Pallas kernels, project_call(): pl.pallas_call(lambda *refs: project_kernel(chunk, outer, inner, cores, *...  6.49 us
  transfers between devices with their start and end apart: 37, of which 9 were waited for; matrix products, arithmetic and copies ran while one was open for 0% of the time, Pallas kernels for 29%

profile of v2, /device:TPU:0, one launch (start us, length us, event | category | flops | bytes accessed | tf_op | source)
XLA Modules:
  0.0 126.8 jit_solution(6485656281004208731)
XLA Ops:
  0.0 2.1 %cut.1 = (bf16[2,2,32,1152]{3,2,1,0:T(8,128)(2,1)}, bf16[72,1024]{1,0:T(8,128)(2,1)}, bf16[72,1024]{1,0:T(8,128)(2,1)}, bf16[72,1024]{1,0:T(8,128)(2,1)}, bf16[72,1024]{1,0:T(8,128)(2,1)}) custom-call(bf16[72,8192]{1,0:T(8,128)(2,1)} %weight_ref.1, bf16[2,8,2,32,1152]{4,3,2,1,0:T(8,128)(2,1)} %bitcast.3), custom_call_target="tpu_custom_call" | custom-call | tf_op jit(solution)/shard_map/cut/pallas_call | solution.py:287
  2.8 2.9 %collective-permute-start.9 = (bf16[72,1024]{1,0:T(8,128)(2,1)}, bf16[72,1024]{1,0:T(8,128)(2,1)S(1)}, u32[]{:S(2)}, u32[]{:S(2)}) collective-permute-start(bf16[72,1024]{1,0:T(8,128)(2,1)} %get-tuple-element.33), channel_id=1, source_target_pairs={{0,2},{1,3},{2,0},{3,1},{4,6},{5,7},{6,4},{7,5},{8,10},{9,11},{10,... | collective-permute-start | bytes 442376 | tf_op jit(solution)/shard_map/ppermute | solution.py:39
  6.5 14.2 %block_last.1 = (bf16[128,1152]{1,0:T(8,128)(2,1)}, f32[128,1152]{1,0:T(8,128)}) custom-call(bf16[2,8,2,32,1152]{4,3,2,1,0:T(8,128)(2,1)} %bitcast.4, bf16[2,2,32,1152]{3,2,1,0:T(8,128)(2,1)} %copy-done.2, bf16[2,2,32,1152]{3,2,1,0:T(8,128)(2,1)} %copy-done.2, bf16[3,3,9,128,128]{4,3,2,1,0:T(8,128)(2,1)} %refs_3_.3, bf16[1152,1152]{1,0:T(8,128)(2,1)} %refs_4_.3, ...), custom_call_target="tpu_custom_call" | custom-call | tf_op jit(solution)/shard_map/block_last/pallas_call | solution.py:211
  22.4 1.6 %collective-permute-start.11 = (bf16[288,1024]{1,0:T(8,128)(2,1)S(1)}, bf16[288,1024]{1,0:T(8,128)(2,1)S(1)}, u32[]{:S(2)}, u32[]{:S(2)}) collective-permute-start(bf16[288,1024]{1,0:T(8,128)(2,1)S(1)} %join.1.refs_4_), channel_id=1, source_target_pairs={{0,4},{2,6},{4,0},{6,2},{8,12},{10,14},{12,8},{14,10},{1,5},{3,7},... | collective-permute-start | bytes 1769480 | tf_op jit(solution)/shard_map/ppermute | solution.py:372
  24.0 14.1 %block_first.1.refs_0_ = f32[128,1152]{1,0:T(8,128)} custom-call(bf16[2,8,2,32,1152]{4,3,2,1,0:T(8,128)(2,1)} %bitcast.5, bf16[2,2,32,1152]{3,2,1,0:T(8,128)(2,1)} %copy-done.2, bf16[2,2,32,1152]{3,2,1,0:T(8,128)(2,1)} %copy-done.2, bf16[3,3,9,128,128]{4,3,2,1,0:T(8,128)(2,1)} %refs_3_.3, bf16[1152,1152]{1,0:T(8,128)(2,1)} %refs_4_.3, ...), custom_call_target="tpu_custom_call" | custom-call | tf_op jit(solution)/shard_map/block_first/pallas_call | solution.py:211
  39.5 2.5 %collective-permute-start.4 = (bf16[32,1152]{1,0:T(8,128)(2,1)S(1)}, bf16[32,1152]{1,0:T(8,128)(2,1)S(1)}, u32[]{:S(2)}, u32[]{:S(2)}) collective-permute-start(bf16[32,1152]{1,0:T(8,128)(2,1)S(1)} %get-tuple-element.56), channel_id=1, source_target_pairs={{0,12},{1,13},{2,14},{3,15},{4,0},{5,1},{6,2},{7,3},{8,4},{9,5},{1... | collective-permute-start | bytes 221192 | tf_op jit(solution)/shard_map/ppermute | solution.py:39
  42.3 1.9 %collective-permute-start.2 = (bf16[32,1152]{1,0:T(8,128)(2,1)S(1)}, bf16[32,1152]{1,0:T(8,128)(2,1)S(1)}, u32[]{:S(2)}, u32[]{:S(2)}) collective-permute-start(bf16[32,1152]{1,0:T(8,128)(2,1)S(1)} %get-tuple-element.58), channel_id=1, source_target_pairs={{0,4},{1,5},{2,6},{3,7},{4,8},{5,9},{6,10},{7,11},{8,12},{9,13},{1... | collective-permute-start | bytes 221192 | tf_op jit(solution)/shard_map/ppermute | solution.py:39
  44.9 5.7 %collective-permute-done.3 = bf16[32,1152]{1,0:T(8,128)(2,1)S(1)} collective-permute-done((bf16[32,1152]{1,0:T(8,128)(2,1)S(1)}, bf16[32,1152]{1,0:T(8,128)(2,1)S(1)}, u32[]{:S(2)}, u32[]{:S(2)}) %collective-permute-start.3) | collective-permute-done | bytes 73760 | tf_op jit(solution)/shard_map/ppermute | solution.py:39
  50.7 2.0 %collective-permute-start.6 = (bf16[128,1152]{1,0:T(8,128)(2,1)S(1)}, bf16[128,1152]{1,0:T(8,128)(2,1)S(1)}, u32[]{:S(2)}, u32[]{:S(2)}) collective-permute-start(bf16[128,1152]{1,0:T(8,128)(2,1)S(1)} %pad_maximum_fusion.refs_0_), channel_id=1, source_target_pairs={{0,2},{1,3},{2,0},{3,1},{4,6},{5,7},{6,4},{7,5},{8,10},{9,11},{10,... | collective-permute-start | bytes 884744 | tf_op jit(solution)/shard_map/ppermute | solution.py:39
  55.8 4.6 %collective-permute-done.6.refs_2_ = bf16[128,1152]{1,0:T(8,128)(2,1)S(1)} collective-permute-done((bf16[128,1152]{1,0:T(8,128)(2,1)S(1)}, bf16[128,1152]{1,0:T(8,128)(2,1)S(1)}, u32[]{:S(2)}, u32[]{:S(2)}) %collective-permute-start.6) | collective-permute-done | bytes 294944 | tf_op jit(solution)/shard_map/ppermute | solution.py:39
  60.3 8.9 %collective-permute-start.13 = (bf16[288,512]{1,0:T(8,128)(2,1)S(1)}, bf16[288,512]{1,0:T(8,128)(2,1)S(1)}, u32[]{:S(2)}, u32[]{:S(2)}) collective-permute-start(bf16[288,512]{1,0:T(8,128)(2,1)S(1)} %get-tuple-element.54), channel_id=1, source_target_pairs={{0,4},{2,6},{4,0},{6,2},{8,12},{10,14},{12,8},{14,10},{1,5},{3,7},... | collective-permute-start | bytes 884744 | tf_op jit(solution)/shard_map/ppermute | solution.py:372
  69.2 5.8 %collective-permute-start.15 = (bf16[288,512]{1,0:T(8,128)(2,1)S(1)}, bf16[288,512]{1,0:T(8,128)(2,1)S(1)}, u32[]{:S(2)}, u32[]{:S(2)}) collective-permute-start(bf16[288,512]{1,0:T(8,128)(2,1)S(1)} %collective-permute-done.14.refs_8_), channel_id=1, source_target_pairs={{0,4},{2,6},{4,0},{6,2},{8,12},{10,14},{12,8},{14,10},{1,5},{3,7},... | collective-permute-start | bytes 884744 | tf_op jit(solution)/shard_map/ppermute | solution.py:372
  75.0 5.6 %collective-permute-start.29 = (bf16[288,512]{1,0:T(8,128)(2,1)S(1)}, bf16[288,512]{1,0:T(8,128)(2,1)S(1)}, u32[]{:S(2)}, u32[]{:S(2)}) collective-permute-start(bf16[288,512]{1,0:T(8,128)(2,1)S(1)} %collective-permute-done.28.refs_8_), channel_id=1, source_target_pairs={{0,4},{2,6},{4,0},{6,2},{8,12},{10,14},{12,8},{14,10},{1,5},{3,7},... | collective-permute-start | bytes 884744 | tf_op jit(solution)/shard_map/ppermute | solution.py:372
  81.2 2.2 %collective-permute-done.15.refs_9_ = bf16[288,512]{1,0:T(8,128)(2,1)S(1)} collective-permute-done((bf16[288,512]{1,0:T(8,128)(2,1)S(1)}, bf16[288,512]{1,0:T(8,128)(2,1)S(1)}, u32[]{:S(2)}, u32[]{:S(2)}) %collective-permute-start.15) | collective-permute-done | bytes 294944 | tf_op jit(solution)/shard_map/ppermute | solution.py:372
  85.1 4.6 %collective-permute-done.27.refs_7_ = bf16[288,512]{1,0:T(8,128)(2,1)S(1)} collective-permute-done((bf16[288,512]{1,0:T(8,128)(2,1)S(1)}, bf16[288,512]{1,0:T(8,128)(2,1)S(1)}, u32[]{:S(2)}, u32[]{:S(2)}) %collective-permute-start.27) | collective-permute-done | bytes 294944 | tf_op jit(solution)/shard_map/ppermute | solution.py:372
  89.7 1.9 %collective-permute-start.17 = (bf16[128,512]{1,0:T(8,128)(2,1)S(1)}, bf16[128,512]{1,0:T(8,128)(2,1)S(1)}, u32[]{:S(2)}, u32[]{:S(2)}) collective-permute-start(bf16[128,512]{1,0:T(8,128)(2,1)S(1)} %get-tuple-element.37), channel_id=1, source_target_pairs={{0,2},{1,3},{2,0},{3,1},{4,6},{5,7},{6,4},{7,5},{8,10},{9,11},{10,... | collective-permute-start | bytes 393224 | tf_op jit(solution)/shard_map/ppermute | solution.py:39
  91.6 3.4 %collective-permute-done.29.refs_9_ = bf16[288,512]{1,0:T(8,128)(2,1)S(1)} collective-permute-done((bf16[288,512]{1,0:T(8,128)(2,1)S(1)}, bf16[288,512]{1,0:T(8,128)(2,1)S(1)}, u32[]{:S(2)}, u32[]{:S(2)}) %collective-permute-start.29) | collective-permute-done | bytes 294944 | tf_op jit(solution)/shard_map/ppermute | solution.py:372
  102.1 2.1 %collective-permute-start.35 = (bf16[128,512]{1,0:T(8,128)(2,1)S(1)}, bf16[128,512]{1,0:T(8,128)(2,1)S(1)}, u32[]{:S(2)}, u32[]{:S(2)}) collective-permute-start(bf16[128,512]{1,0:T(8,128)(2,1)S(1)} %get-tuple-element.49), channel_id=1, source_target_pairs={{0,18},{1,19},{2,16},{3,17},{4,22},{5,23},{6,20},{7,21},{8,26},{9,... | collective-permute-start | bytes 393224 | tf_op jit(solution)/shard_map/ppermute | solution.py:39
  109.1 1.7 %collective-permute-start.24 = (bf16[128,512]{1,0:T(8,128)(2,1)S(1)}, bf16[128,512]{1,0:T(8,128)(2,1)S(1)}, u32[]{:S(2)}, u32[]{:S(2)}) collective-permute-start(bf16[128,512]{1,0:T(8,128)(2,1)S(1)} %get-tuple-element.40), channel_id=1, source_target_pairs={{0,17},{1,16},{2,19},{3,18},{4,21},{5,20},{6,23},{7,22},{8,25},{9,... | collective-permute-start | bytes 393224 | tf_op jit(solution)/shard_map/ppermute | solution.py:39
  110.7 2.3 %collective-permute-done.35.refs_6_ = bf16[128,512]{1,0:T(8,128)(2,1)S(1)} collective-permute-done((bf16[128,512]{1,0:T(8,128)(2,1)S(1)}, bf16[128,512]{1,0:T(8,128)(2,1)S(1)}, u32[]{:S(2)}, u32[]{:S(2)}) %collective-permute-start.35) | collective-permute-done | bytes 131104 | tf_op jit(solution)/shard_map/ppermute | solution.py:39
  113.0 1.8 %collective-permute-start.25 = (bf16[128,512]{1,0:T(8,128)(2,1)S(1)}, bf16[128,512]{1,0:T(8,128)(2,1)S(1)}, u32[]{:S(2)}, u32[]{:S(2)}) collective-permute-start(bf16[128,512]{1,0:T(8,128)(2,1)S(1)} %get-tuple-element.41), channel_id=1, source_target_pairs={{0,18},{1,19},{2,16},{3,17},{4,22},{5,23},{6,20},{7,21},{8,26},{9,... | collective-permute-start | bytes 393224 | tf_op jit(solution)/shard_map/ppermute | solution.py:39
  114.8 2.2 %collective-permute-start.26 = (bf16[128,512]{1,0:T(8,128)(2,1)S(1)}, bf16[128,512]{1,0:T(8,128)(2,1)S(1)}, u32[]{:S(2)}, u32[]{:S(2)}) collective-permute-start(bf16[128,512]{1,0:T(8,128)(2,1)S(1)} %get-tuple-element.42), channel_id=1, source_target_pairs={{0,19},{1,18},{2,17},{3,16},{4,23},{5,22},{6,21},{7,20},{8,27},{9,... | collective-permute-start | bytes 393224 | tf_op jit(solution)/shard_map/ppermute | solution.py:39
  118.1 1.8 %collective-permute-done.24.refs_5_ = bf16[128,512]{1,0:T(8,128)(2,1)S(1)} collective-permute-done((bf16[128,512]{1,0:T(8,128)(2,1)S(1)}, bf16[128,512]{1,0:T(8,128)(2,1)S(1)}, u32[]{:S(2)}, u32[]{:S(2)}) %collective-permute-start.24) | collective-permute-done | bytes 131104 | tf_op jit(solution)/shard_map/ppermute | solution.py:39
  119.8 4.4 %collective-permute-done.25.refs_6_ = bf16[128,512]{1,0:T(8,128)(2,1)S(1)} collective-permute-done((bf16[128,512]{1,0:T(8,128)(2,1)S(1)}, bf16[128,512]{1,0:T(8,128)(2,1)S(1)}, u32[]{:S(2)}, u32[]{:S(2)}) %collective-permute-start.25) | collective-permute-done | bytes 131104 | tf_op jit(solution)/shard_map/ppermute | solution.py:39
  (76 shorter events, 26.2 us)
Async XLA Ops:
  2.7 19.6 %collective-permute-start.8 = (bf16[72,1024]{1,0:T(8,128)(2,1)}, bf16[72,1024]{1,0:T(8,128)(2,1)S(1)}, u32[]{:S(2)}, u32[]{:S(2)}) collective-permute-start(bf16[72,1024]{1,0:T(8,128)(2,1)} %get-tuple-element.32), channel_id=1, source_target_pairs={{0,1},{1,0},{2,3},{3,2},{4,5},{5,4},{6,7},{7,6},{8,9},{9,8},{10,11... | collective-permute-start | bytes 442376 | tf_op jit(solution)/shard_map/ppermute | solution.py:39
  2.8 19.5 %collective-permute-start.9 = (bf16[72,1024]{1,0:T(8,128)(2,1)}, bf16[72,1024]{1,0:T(8,128)(2,1)S(1)}, u32[]{:S(2)}, u32[]{:S(2)}) collective-permute-start(bf16[72,1024]{1,0:T(8,128)(2,1)} %get-tuple-element.33), channel_id=1, source_target_pairs={{0,2},{1,3},{2,0},{3,1},{4,6},{5,7},{6,4},{7,5},{8,10},{9,11},{10,... | collective-permute-start | bytes 442376 | tf_op jit(solution)/shard_map/ppermute | solution.py:39
  5.7 16.6 %collective-permute-start.10 = (bf16[72,1024]{1,0:T(8,128)(2,1)}, bf16[72,1024]{1,0:T(8,128)(2,1)S(1)}, u32[]{:S(2)}, u32[]{:S(2)}) collective-permute-start(bf16[72,1024]{1,0:T(8,128)(2,1)} %get-tuple-element.34), channel_id=1, source_target_pairs={{0,3},{1,2},{2,1},{3,0},{4,7},{5,6},{6,5},{7,4},{8,11},{9,10},{10,... | collective-permute-start | bytes 442376 | tf_op jit(solution)/shard_map/ppermute | solution.py:39
  20.7 17.4 %collective-permute-start.1 = (bf16[128,1152]{1,0:T(8,128)(2,1)}, bf16[128,1152]{1,0:T(8,128)(2,1)S(1)}, u32[]{:S(2)}, u32[]{:S(2)}) collective-permute-start(bf16[128,1152]{1,0:T(8,128)(2,1)} %get-tuple-element.30), channel_id=1, source_target_pairs={{0,2},{2,4},{4,6},{6,8},{8,10},{10,12},{12,14},{14,0},{1,3},{3,5},... | collective-permute-start | bytes 884744 | tf_op jit(solution)/shard_map/ppermute | solution.py:603
  22.4 31.9 %collective-permute-start.11 = (bf16[288,1024]{1,0:T(8,128)(2,1)S(1)}, bf16[288,1024]{1,0:T(8,128)(2,1)S(1)}, u32[]{:S(2)}, u32[]{:S(2)}) collective-permute-start(bf16[288,1024]{1,0:T(8,128)(2,1)S(1)} %join.1.refs_4_), channel_id=1, source_target_pairs={{0,4},{2,6},{4,0},{6,2},{8,12},{10,14},{12,8},{14,10},{1,5},{3,7},... | collective-permute-start | bytes 1769480 | tf_op jit(solution)/shard_map/ppermute | solution.py:372
  52.7 16.5 %collective-permute-start.19 = (bf16[128,1152]{1,0:T(8,128)(2,1)S(1)}, bf16[128,1152]{1,0:T(8,128)(2,1)S(1)}, u32[]{:S(2)}, u32[]{:S(2)}) collective-permute-start(bf16[128,1152]{1,0:T(8,128)(2,1)S(1)} %pad_maximum_fusion.refs_0_), channel_id=1, source_target_pairs={{0,16},{1,17},{2,18},{3,19},{4,20},{5,21},{6,22},{7,23},{8,24},{9,... | collective-permute-start | bytes 884744 | tf_op jit(solution)/shard_map/ppermute | solution.py:39
  54.3 20.7 %collective-permute-start.21 = (bf16[128,1152]{1,0:T(8,128)(2,1)S(1)}, bf16[128,1152]{1,0:T(8,128)(2,1)S(1)}, u32[]{:S(2)}, u32[]{:S(2)}) collective-permute-start(bf16[128,1152]{1,0:T(8,128)(2,1)S(1)} %pad_maximum_fusion.refs_0_), channel_id=1, source_target_pairs={{0,18},{1,19},{2,16},{3,17},{4,22},{5,23},{6,20},{7,21},{8,26},{9,... | collective-permute-start | bytes 884744 | tf_op jit(solution)/shard_map/ppermute | solution.py:39
  54.3 14.9 %collective-permute-start.14 = (bf16[288,512]{1,0:T(8,128)(2,1)S(1)}, bf16[288,512]{1,0:T(8,128)(2,1)S(1)}, u32[]{:S(2)}, u32[]{:S(2)}) collective-permute-start(bf16[288,512]{1,0:T(8,128)(2,1)S(1)} %get-tuple-element.52), channel_id=1, source_target_pairs={{0,0},{2,2},{4,8},{6,10},{8,4},{10,6},{12,12},{14,14},{1,1},{3,3},... | collective-permute-start | bytes 884744 | tf_op jit(solution)/shard_map/ppermute | solution.py:372
  55.0 20.0 %collective-permute-start.28 = (bf16[288,512]{1,0:T(8,128)(2,1)S(1)}, bf16[288,512]{1,0:T(8,128)(2,1)S(1)}, u32[]{:S(2)}, u32[]{:S(2)}) collective-permute-start(bf16[288,512]{1,0:T(8,128)(2,1)S(1)} %get-tuple-element.51), channel_id=1, source_target_pairs={{0,0},{2,2},{4,8},{6,10},{8,4},{10,6},{12,12},{14,14},{1,1},{3,3},... | collective-permute-start | bytes 884744 | tf_op jit(solution)/shard_map/ppermute | solution.py:372
  60.3 20.3 %collective-permute-start.13 = (bf16[288,512]{1,0:T(8,128)(2,1)S(1)}, bf16[288,512]{1,0:T(8,128)(2,1)S(1)}, u32[]{:S(2)}, u32[]{:S(2)}) collective-permute-start(bf16[288,512]{1,0:T(8,128)(2,1)S(1)} %get-tuple-element.54), channel_id=1, source_target_pairs={{0,4},{2,6},{4,0},{6,2},{8,12},{10,14},{12,8},{14,10},{1,5},{3,7},... | collective-permute-start | bytes 884744 | tf_op jit(solution)/shard_map/ppermute | solution.py:372
  69.2 11.4 %collective-permute-start.7 = (bf16[128,1152]{1,0:T(8,128)(2,1)S(1)}, bf16[128,1152]{1,0:T(8,128)(2,1)S(1)}, u32[]{:S(2)}, u32[]{:S(2)}) collective-permute-start(bf16[128,1152]{1,0:T(8,128)(2,1)S(1)} %collective-permute-done.6.refs_2_), channel_id=1, source_target_pairs={{0,1},{1,0},{2,3},{3,2},{4,5},{5,4},{6,7},{7,6},{8,9},{9,8},{10,11... | collective-permute-start | bytes 884744 | tf_op jit(solution)/shard_map/ppermute | solution.py:39
  69.2 14.2 %collective-permute-start.15 = (bf16[288,512]{1,0:T(8,128)(2,1)S(1)}, bf16[288,512]{1,0:T(8,128)(2,1)S(1)}, u32[]{:S(2)}, u32[]{:S(2)}) collective-permute-start(bf16[288,512]{1,0:T(8,128)(2,1)S(1)} %collective-permute-done.14.refs_8_), channel_id=1, source_target_pairs={{0,4},{2,6},{4,0},{6,2},{8,12},{10,14},{12,8},{14,10},{1,5},{3,7},... | collective-permute-start | bytes 884744 | tf_op jit(solution)/shard_map/ppermute | solution.py:372
  75.0 14.7 %collective-permute-start.27 = (bf16[288,512]{1,0:T(8,128)(2,1)S(1)}, bf16[288,512]{1,0:T(8,128)(2,1)S(1)}, u32[]{:S(2)}, u32[]{:S(2)}) collective-permute-start(bf16[288,512]{1,0:T(8,128)(2,1)S(1)} %get-tuple-element.53), channel_id=1, source_target_pairs={{0,4},{2,6},{4,0},{6,2},{8,12},{10,14},{12,8},{14,10},{1,5},{3,7},... | collective-permute-start | bytes 884744 | tf_op jit(solution)/shard_map/ppermute | solution.py:372
  75.0 20.0 %collective-permute-start.29 = (bf16[288,512]{1,0:T(8,128)(2,1)S(1)}, bf16[288,512]{1,0:T(8,128)(2,1)S(1)}, u32[]{:S(2)}, u32[]{:S(2)}) collective-permute-start(bf16[288,512]{1,0:T(8,128)(2,1)S(1)} %collective-permute-done.28.refs_8_), channel_id=1, source_target_pairs={{0,4},{2,6},{4,0},{6,2},{8,12},{10,14},{12,8},{14,10},{1,5},{3,7},... | collective-permute-start | bytes 884744 | tf_op jit(solution)/shard_map/ppermute | solution.py:372
  80.6 16.1 %collective-permute-start.20 = (bf16[128,1152]{1,0:T(8,128)(2,1)S(1)}, bf16[128,1152]{1,0:T(8,128)(2,1)S(1)}, u32[]{:S(2)}, u32[]{:S(2)}) collective-permute-start(bf16[128,1152]{1,0:T(8,128)(2,1)S(1)} %collective-permute-done.19.refs_0_), channel_id=1, source_target_pairs={{0,1},{1,0},{2,3},{3,2},{4,5},{5,4},{6,7},{7,6},{8,9},{9,8},{10,11... | collective-permute-start | bytes 884744 | tf_op jit(solution)/shard_map/ppermute | solution.py:39
  80.6 17.4 %collective-permute-start.22 = (bf16[128,1152]{1,0:T(8,128)(2,1)S(1)}, bf16[128,1152]{1,0:T(8,128)(2,1)S(1)}, u32[]{:S(2)}, u32[]{:S(2)}) collective-permute-start(bf16[128,1152]{1,0:T(8,128)(2,1)S(1)} %collective-permute-done.21.refs_2_), channel_id=1, source_target_pairs={{0,1},{1,0},{2,3},{3,2},{4,5},{5,4},{6,7},{7,6},{8,9},{9,8},{10,11... | collective-permute-start | bytes 884744 | tf_op jit(solution)/shard_map/ppermute | solution.py:39
  85.0 15.2 %collective-permute-start.16 = (bf16[128,512]{1,0:T(8,128)(2,1)S(1)}, bf16[128,512]{1,0:T(8,128)(2,1)S(1)}, u32[]{:S(2)}, u32[]{:S(2)}) collective-permute-start(bf16[128,512]{1,0:T(8,128)(2,1)S(1)} %get-tuple-element.36), channel_id=1, source_target_pairs={{0,1},{1,0},{2,3},{3,2},{4,5},{5,4},{6,7},{7,6},{8,9},{9,8},{10,11... | collective-permute-start | bytes 393224 | tf_op jit(solution)/shard_map/ppermute | solution.py:39
  89.7 12.1 %collective-permute-start.17 = (bf16[128,512]{1,0:T(8,128)(2,1)S(1)}, bf16[128,512]{1,0:T(8,128)(2,1)S(1)}, u32[]{:S(2)}, u32[]{:S(2)}) collective-permute-start(bf16[128,512]{1,0:T(8,128)(2,1)S(1)} %get-tuple-element.37), channel_id=1, source_target_pairs={{0,2},{1,3},{2,0},{3,1},{4,6},{5,7},{6,4},{7,5},{8,10},{9,11},{10,... | collective-permute-start | bytes 393224 | tf_op jit(solution)/shard_map/ppermute | solution.py:39
  102.1 10.9 %collective-permute-start.35 = (bf16[128,512]{1,0:T(8,128)(2,1)S(1)}, bf16[128,512]{1,0:T(8,128)(2,1)S(1)}, u32[]{:S(2)}, u32[]{:S(2)}) collective-permute-start(bf16[128,512]{1,0:T(8,128)(2,1)S(1)} %get-tuple-element.49), channel_id=1, source_target_pairs={{0,18},{1,19},{2,16},{3,17},{4,22},{5,23},{6,20},{7,21},{8,26},{9,... | collective-permute-start | bytes 393224 | tf_op jit(solution)/shard_map/ppermute | solution.py:39
  104.1 10.7 %collective-permute-start.36 = (bf16[128,512]{1,0:T(8,128)(2,1)S(1)}, bf16[128,512]{1,0:T(8,128)(2,1)S(1)}, u32[]{:S(2)}, u32[]{:S(2)}) collective-permute-start(bf16[128,512]{1,0:T(8,128)(2,1)S(1)} %get-tuple-element.50), channel_id=1, source_target_pairs={{0,19},{1,18},{2,17},{3,16},{4,23},{5,22},{6,21},{7,20},{8,27},{9,... | collective-permute-start | bytes 393224 | tf_op jit(solution)/shard_map/ppermute | solution.py:39
  106.4 11.7 %collective-permute-start.18 = (bf16[128,512]{1,0:T(8,128)(2,1)S(1)}, bf16[128,512]{1,0:T(8,128)(2,1)S(1)}, u32[]{:S(2)}, u32[]{:S(2)}) collective-permute-start(bf16[128,512]{1,0:T(8,128)(2,1)S(1)} %get-tuple-element.38), channel_id=1, source_target_pairs={{0,3},{1,2},{2,1},{3,0},{4,7},{5,6},{6,5},{7,4},{8,11},{9,10},{10,... | collective-permute-start | bytes 393224 | tf_op jit(solution)/shard_map/ppermute | solution.py:39
  109.1 10.7 %collective-permute-start.24 = (bf16[128,512]{1,0:T(8,128)(2,1)S(1)}, bf16[128,512]{1,0:T(8,128)(2,1)S(1)}, u32[]{:S(2)}, u32[]{:S(2)}) collective-permute-start(bf16[128,512]{1,0:T(8,128)(2,1)S(1)} %get-tuple-element.40), channel_id=1, source_target_pairs={{0,17},{1,16},{2,19},{3,18},{4,21},{5,20},{6,23},{7,22},{8,25},{9,... | collective-permute-start | bytes 393224 | tf_op jit(solution)/shard_map/ppermute | solution.py:39
  113.0 11.2 %collective-permute-start.25 = (bf16[128,512]{1,0:T(8,128)(2,1)S(1)}, bf16[128,512]{1,0:T(8,128)(2,1)S(1)}, u32[]{:S(2)}, u32[]{:S(2)}) collective-permute-start(bf16[128,512]{1,0:T(8,128)(2,1)S(1)} %get-tuple-element.41), channel_id=1, source_target_pairs={{0,18},{1,19},{2,16},{3,17},{4,22},{5,23},{6,20},{7,21},{8,26},{9,... | collective-permute-start | bytes 393224 | tf_op jit(solution)/shard_map/ppermute | solution.py:39
  114.8 11.0 %collective-permute-start.26 = (bf16[128,512]{1,0:T(8,128)(2,1)S(1)}, bf16[128,512]{1,0:T(8,128)(2,1)S(1)}, u32[]{:S(2)}, u32[]{:S(2)}) collective-permute-start(bf16[128,512]{1,0:T(8,128)(2,1)S(1)} %get-tuple-element.42), channel_id=1, source_target_pairs={{0,19},{1,18},{2,17},{3,16},{4,23},{5,22},{6,21},{7,20},{8,27},{9,... | collective-permute-start | bytes 393224 | tf_op jit(solution)/shard_map/ppermute | solution.py:39
  (17 other events, 130.9 us)
